TPU v7x, 32 devices: a 4x4x1 block of a 4x4x8 slice. The times are simulated.
32 devices in a mesh: rep: 1 (over z), dp: 32 (over x, y, core).
Axes of the slice: x: 4, y: 4, z: 1, core: 2. Of those that a mesh axis runs over, the one named last changes fastest.
The devices are a block of a 4x4x8 slice.
Arguments:
- x: bfloat16 [32, 2048, 1024], P(('rep', 'dp'))
- dy: bfloat16 [32, 2048, 1024], P(('rep', 'dp'))
- w_gate: bfloat16 [2, 1024, 2560], replicated
- w_up: bfloat16 [2, 1024, 2560], replicated
- w_down: bfloat16 [2, 2560, 1024], replicated
- m_w_gate: float32 [2, 1024, 2560], replicated
- m_w_up: float32 [2, 1024, 2560], replicated
- m_w_down: float32 [2, 2560, 1024], replicated
- v_w_gate: float32 [2, 1024, 2560], replicated
- v_w_up: float32 [2, 1024, 2560], replicated
- v_w_down: float32 [2, 2560, 1024], replicated
Outputs:
- output 1: bfloat16 [2, 1024, 2560], P('rep')
- output 2: bfloat16 [2, 1024, 2560], P('rep')
- output 3: bfloat16 [2, 2560, 1024], P('rep')
- output 4: float32 [2, 1024, 2560], P('rep')
- output 5: float32 [2, 1024, 2560], P('rep')
- output 6: float32 [2, 2560, 1024], P('rep')
- output 7: float32 [2, 1024, 2560], P('rep')
- output 8: float32 [2, 1024, 2560], P('rep')
- output 9: float32 [2, 2560, 1024], P('rep')
All inputs are finite; a program needn't handle non-finite values.
Results may differ from a plain program's by a relative error of at most 0.022.
Values are sent between devices in bfloat16 or wider.
A program may use at most 768 MiB of HBM per device.

v0:
```python
import jax
import jax.numpy as jnp
from jax import lax
from jax.sharding import PartitionSpec as P

NAMES = ("w_gate", "w_up", "w_down")


def matmul(a, w):
    return jnp.dot(a, w, preferred_element_type=jnp.float32).astype(jnp.bfloat16)


def normed(h):
    wide = h.astype(jnp.float32)
    scale = lax.rsqrt(jnp.mean(wide**2, -1, keepdims=True) + 1e-6)
    return (wide * scale).astype(jnp.bfloat16)


def layer(h, w):
    a = normed(h)
    gate = jnp.dot(a, w["w_gate"], preferred_element_type=jnp.float32)
    up = jnp.dot(a, w["w_up"], preferred_element_type=jnp.float32)
    return h + matmul((jax.nn.silu(gate) * up).astype(jnp.bfloat16), w["w_down"])


def adamw(w, m, v, g):
    m = 0.9 * m + 0.1 * g
    v = 0.95 * v + 0.05 * g * g
    step = m * lax.rsqrt(v + 1e-8) + 0.1 * w
    return (w - 0.02 * step).astype(jnp.bfloat16), m, v


def clipped(gradients, sum_of_squares, count):
    factor = jnp.minimum(1.0, 0.5 * lax.rsqrt(sum_of_squares / count + 1e-30))
    return [g * factor for g in gradients]


def solution(mesh):
    def step(x, dy, *arrays):
        weights, m, v = (arrays[i : i + 3] for i in (0, 3, 6))
        layers = weights[0].shape[0]
        h, kept = x[0], []
        for number in range(layers):
            kept.append(h)
            h = layer(h, {name: w[number] for name, w in zip(NAMES, weights, strict=True)})
        by_h, summed = dy[0], [None] * layers
        for number in reversed(range(layers)):
            _, back = jax.vjp(lambda w, h: layer(h, w), {name: w[number] for name, w in zip(NAMES, weights, strict=True)}, kept[number])
            by_w, by_h = back(by_h)
            summed[number] = [lax.psum(by_w[name], "dp") for name in NAMES]
        gradients = [jnp.stack([summed[number][i] for number in range(layers)]).astype(jnp.float32) for i in range(3)]
        gradients = clipped(gradients, sum(jnp.sum(g * g) for g in gradients), sum(g.size for g in gradients))
        new = [adamw(w.astype(jnp.float32), m, v, g) for w, m, v, g in zip(weights, m, v, gradients, strict=True)]
        return tuple(one[which] for which in range(3) for one in new)

    return jax.shard_map(
        step,
        mesh=mesh,
        in_specs=(P(("rep", "dp"), None, None),) * 2 + (P(None, None, None),) * 9,
        out_specs=(P("rep", None, None),) * 9,
        check_vma=False,
    )
```

profile of v0, /device:TPU:97, one launch (start us, length us, event | category | flops | bytes accessed | tf_op | source)
XLA Modules:
  0.0 697.2 jit_solution(10637517939215729689)
XLA Ops:
  7.2 0.1 all-reduce.3.cloned.1.call-start
  7.3 6.5 copy.20
  13.7 3.1 fusion.36
  16.8 0.0 copy-start.7
  16.8 0.0 slice-start.2
  16.8 6.7 copy.21
  23.5 0.0 slice-start.3
  23.5 0.0 slice-start.4
  23.5 0.0 copy-start.4
  23.5 16.9 %convolution_convert_fusion.1 = bf16[2048,2560]{1,0:T(8,128)(2,1)} fusion(bf16[2,2560,1024]{2,1,0:T(8,128)(2,1)} %param.15, bf16[1,2048,1024]{2,1,0:T(8,128)(2,1)} %param.12), kind=kOutput, calls=%fused_computation.63 | convolution fusion | flops 10742661120 | bytes 19922944 | tf_op jit(solution)/shard_map/transpose(jvp())/dot_general | solution.py:10
  40.4 0.0 slice-done.2
  40.4 0.0 slice-done.3
  40.4 0.0 slice-done.4
  40.4 0.0 copy-done.4
  40.4 14.1 %fusion.62 = f32[2048,2560]{1,0:T(8,128)} fusion(bf16[2,1024,2560]{2,1,0:T(8,128)(2,1)S(1)} %bitcast.77, bf16[1,2048,1024]{2,1,0:T(8,128)(2,1)S(1)} %copy-done.4, f32[2048]{0:T(1024)S(1)} %add_rsqrt_fusion), kind=kOutput, calls=%fused_computation.99 | convolution fusion | flops 10743709696 | bytes 30416896 | tf_op jit(solution)/shard_map/dot_general | solution.py:21
  54.6 0.0 copy-done.7
  54.6 0.0 copy-start.2
  54.6 26.7 %multiply_convert_fusion.1 = (bf16[2048,2560]{1,0:T(8,128)(2,1)}, f32[2048,2560]{1,0:T(8,128)}) fusion(f32[2048,2560]{1,0:T(8,128)} %fusion.62, bf16[2,1024,2560]{2,1,0:T(8,128)(2,1)} %param.14, bf16[1,2048,1024]{2,1,0:T(8,128)(2,1)} %param.11, f32[2048]{0:T(1024)S(1)} %add_rsqrt_fusion), kind=kOutput, calls=%fused_computation.53 | convolution fusion | flops 10775166976 | bytes 61874176 | tf_op jit(solution)/shard_map/dot_general | solution.py:22
  81.3 0.0 copy-done.2
  81.3 17.7 %fusion.40 = (f32[2048]{0:T(1024)S(1)}, bf16[2048,1024]{0,1:T(8,128)(2,1)}) fusion(bf16[2048,2560]{1,0:T(8,128)(2,1)} %get-tuple-element.24, bf16[2,2560,1024]{2,1,0:T(8,128)(2,1)} %param.15, bf16[1,2048,1024]{1,2,0:T(8,128)(2,1)S(1)} %copy-done.2), kind=kOutput, calls=%fused_computation.76 | convolution fusion | flops 10747901952 | bytes 24125440 | tf_op jit(solution)/shard_map/dot_general | solution.py:10
  98.9 0.0 copy-start.5
  99.0 18.5 %fusion.49 = f32[2048,2560]{1,0:T(8,128)} fusion(bf16[2,1024,2560]{2,1,0:T(8,128)(2,1)} %param.14, bf16[2048,1024]{0,1:T(8,128)(2,1)} %get-tuple-element.27, f32[2048]{0:T(1024)S(1)} %fusion.98), kind=kOutput, calls=%fused_computation.86 | convolution fusion | flops 10743709696 | bytes 30416896 | tf_op jit(solution)/shard_map/jvp()/dot_general | solution.py:22
  117.4 0.0 copy-done.5
  117.4 32.4 %fusion.20 = (bf16[2048,2560]{1,0:T(8,128)(2,1)}, f32[2048,2560]{1,0:T(8,128)}) fusion(f32[2048,2560]{1,0:T(8,128)} %fusion.49, bf16[2048,2560]{1,0:T(8,128)(2,1)} %convolution_convert_fusion.1, bf16[2,1024,2560]{2,1,0:T(8,128)(2,1)} %param.13, bf16[2048,1024]{0,1:T(8,128)(2,1)} %get-tuple-element.27, f32[2048]{0:T(1024)S(1)} %fusion.98), kind=kOutput, calls=%fused_computation.41 | convolution fusion | flops 10806624256 | bytes 72359936 | tf_op jit(solution)/shard_map/jvp()/dot_general | solution.py:21
  149.8 19.9 %fusion.33 = bf16[2048,1024]{0,1:T(8,128)(2,1)} fusion(bf16[2048,2560]{1,0:T(8,128)(2,1)} %convolution_convert_fusion.1, bf16[2,1024,2560]{2,1,0:T(8,128)(2,1)} %param.14, f32[2048,2560]{1,0:T(8,128)} %get-tuple-element.29), kind=kOutput, calls=%fused_computation.61 | convolution fusion | flops 10768875520 | bytes 40894464 | tf_op jit(solution)/shard_map/transpose(jvp())/dot_general | solution.py:22
  169.8 20.0 %fusion.71 = bf16[1,1024,2560]{2,1,0:T(8,128)(2,1)} fusion(bf16[2048,2560]{1,0:T(8,128)(2,1)} %convolution_convert_fusion.1, bf16[2048,1024]{0,1:T(8,128)(2,1)} %get-tuple-element.27, f32[2048]{0:T(1024)S(1)} %fusion.98, f32[2048,2560]{1,0:T(8,128)} %get-tuple-element.29), kind=kOutput, calls=%fused_computation.106 | convolution fusion | flops 10777788416 | bytes 40902656 | tf_op jit(solution)/shard_map/transpose(jvp())/dot_general | solution.py:22
  189.7 22.1 %fusion.72 = bf16[1,2560,1024]{2,1,0:T(8,128)(2,1)} fusion(f32[2048,2560]{1,0:T(8,128)} %fusion.49, bf16[1,2048,1024]{2,1,0:T(8,128)(2,1)} %param.12, f32[2048,2560]{1,0:T(8,128)} %get-tuple-element.29), kind=kOutput, calls=%fused_computation.107 | convolution fusion | flops 10771496960 | bytes 51380224 | tf_op jit(solution)/shard_map/transpose(jvp())/dot_general | solution.py:10
  211.9 0.0 copy-start.3
  211.9 16.6 %fusion.73 = bf16[1,1024,2560]{2,1,0:T(8,128)(2,1)} fusion(bf16[2048,2560]{1,0:T(8,128)(2,1)} %get-tuple-element.28, bf16[2048,1024]{0,1:T(8,128)(2,1)} %get-tuple-element.27, f32[2048]{0:T(1024)S(1)} %fusion.98), kind=kOutput, calls=%fused_computation.108 | convolution fusion | flops 10743709696 | bytes 19931136 | tf_op jit(solution)/shard_map/transpose(jvp())/dot_general | solution.py:21
  228.4 0.0 copy-done.3
  228.4 0.0 copy-start.6
  228.4 0.0 copy-start.1
  228.4 16.8 %fusion.42 = (f32[2048]{0:T(1024)S(1)}, bf16[2048,1024]{0,1:T(8,128)(2,1)S(1)}) fusion(bf16[2048,1024]{0,1:T(8,128)(2,1)S(1)} %copy-done.3, bf16[2048,1024]{0,1:T(8,128)(2,1)} %fusion.33, bf16[2048,2560]{1,0:T(8,128)(2,1)} %get-tuple-element.28, bf16[2,1024,2560]{2,1,0:T(8,128)(2,1)} %param.13), kind=kOutput, calls=%fused_computation.78 | convolution fusion | flops 10747901952 | bytes 28319744 | tf_op jit(solution)/shard_map/transpose(jvp())/dot_general | solution.py:21
  245.3 0.0 copy-done.6
  245.3 0.0 copy-done.1
  245.3 3.2 fusion.82
  248.5 15.8 %convolution_convert_fusion = bf16[2048,2560]{1,0:T(8,128)(2,1)} fusion(bf16[2048,1024]{0,1:T(8,128)(2,1)S(1)} %fusion.82, bf16[2,2560,1024]{2,1,0:T(8,128)(2,1)} %param.15), kind=kOutput, calls=%fused_computation.62 | convolution fusion | flops 10742661120 | bytes 19922944 | tf_op jit(solution)/shard_map/transpose(jvp())/dot_general | solution.py:10
  264.3 0.0 copy-start.8
  264.3 15.6 %fusion.74 = bf16[1,2560,1024]{2,1,0:T(8,128)(2,1)} fusion(bf16[2048,2560]{1,0:T(8,128)(2,1)} %get-tuple-element.24, bf16[2048,1024]{0,1:T(8,128)(2,1)S(1)} %fusion.82), kind=kOutput, calls=%fused_computation.109 | convolution fusion | flops 10740039680 | bytes 19922944 | tf_op jit(solution)/shard_map/transpose(jvp())/dot_general | solution.py:10
  279.9 0.0 copy-done.8
  279.9 20.1 %fusion.67 = bf16[1,1024,2560]{2,1,0:T(8,128)(2,1)} fusion(bf16[2048,2560]{1,0:T(8,128)(2,1)} %convolution_convert_fusion, bf16[1,2048,1024]{1,2,0:T(8,128)(2,1)} %copy.20, f32[2048]{0:T(1024)S(1)} %copy-done.8, f32[2048,2560]{1,0:T(8,128)} %fusion.62), kind=kOutput, calls=%fused_computation.104 | convolution fusion | flops 10777788416 | bytes 40902656 | tf_op jit(solution)/shard_map/transpose(jvp())/dot_general | solution.py:22
  300.0 24.9 %fusion.68 = bf16[1,1024,2560]{2,1,0:T(8,128)(2,1)} fusion(f32[2048,2560]{1,0:T(8,128)} %fusion.62, f32[2048,2560]{1,0:T(8,128)} %get-tuple-element.25, bf16[2048,2560]{1,0:T(8,128)(2,1)} %convolution_convert_fusion, bf16[1,2048,1024]{1,2,0:T(8,128)(2,1)} %copy.20, f32[2048]{0:T(1024)S(1)} %copy-done.8), kind=kOutput, calls=%fused_computation.105 | convolution fusion | flops 10804002816 | bytes 61874176 | tf_op jit(solution)/shard_map/transpose(jvp())/dot_general | solution.py:21
  324.9 0.1 all-reduce.3.cloned.1.call-update
  324.9 225.9 %all-reduce.3.cloned.1.call-done = (bf16[1,1024,2560]{2,1,0:T(8,128)(2,1)}, bf16[1,1024,2560]{2,1,0:T(8,128)(2,1)}, bf16[1,1024,2560]{2,1,0:T(8,128)(2,1)}, bf16...) async-done(((bf16[1,1024,2560]{2,1,0:T(8,128)(2,1)}, bf16[1,1024,2560]{2,1,0:T(8,128)(2,1)}, ...) | async-done | bytes 31457296 | tf_op jit(solution)/shard_map/psum | solution.py:50
  550.9 0.0 slice-start
  550.9 0.0 copy-start
  550.9 0.0 slice-start.1
  550.9 9.4 %fusion.10 = f32[]{:T(128)} fusion(bf16[1,1024,2560]{2,1,0:T(8,128)(2,1)} %get-tuple-element.9, bf16[1,1024,2560]{2,1,0:T(8,128)(2,1)} %get-tuple-element.10), kind=kLoop, calls=%fused_computation.31 | loop fusion | flops 20971520 | bytes 10485764 | tf_op jit(solution)/shard_map/reduce_sum | solution.py:52
  560.3 0.0 slice-done
  560.3 0.0 copy-done
  560.3 0.0 slice-done.1
  560.3 6.0 fusion.11
  567.7 8.5 %fusion.12 = f32[]{:T(128)} fusion(bf16[1,2560,1024]{2,1,0:T(8,128)(2,1)} %get-tuple-element.13, bf16[1,2560,1024]{2,1,0:T(8,128)(2,1)} %get-tuple-element.14), kind=kLoop, calls=%fused_computation.33 | loop fusion | flops 20971520 | bytes 10485764 | tf_op jit(solution)/shard_map/reduce_sum | solution.py:52
  576.9 40.2 %fusion.18 = (bf16[2,2560,1024]{2,1,0:T(8,128)(2,1)}, f32[2,2560,1024]{2,1,0:T(8,128)}, f32[2,2560,1024]{2,1,0:T(8,128)}) fusion(bf16[2,2560,1024]{2,1,0:T(8,128)(2,1)} %param.15, f32[]{:T(128)S(6)} %min_shard_map.3, bf16[1,2560,1024]{2,1,0:T(8,128)(2,1)} %get-tuple-element.13, bf16[1,2560,1024]{2,1,0:T(8,128)(2,1)} %get-tuple-element.14, ...), kind=kLoop, calls=%fused_computation.39 | loop fusion | flops 104857600 | bytes 115343360 | tf_op jit(solution)/shard_map/convert_element_type | solution.py:30
  617.1 72.8 %fusion.8 = (bf16[2,1024,2560]{2,1,0:T(8,128)(2,1)}, f32[2,1024,2560]{2,1,0:T(8,128)}, f32[2,1024,2560]{2,1,0:T(8,128)}, bf16[2,1024,2560]{2,1,0:T(8,128)(2,1)},...) fusion(bf16[2,1024,2560]{2,1,0:T(8,128)(2,1)} %param.13, f32[]{:T(128)S(6)} %min_shard_map.3, ...), kind=kLoop, calls=%fused_computation.29 | loop fusion | flops 209715200 | bytes 230686720 | tf_op jit(solution)/shard_map/convert_element_type | solution.py:30
  (5 shorter events, 0.0 us)
Async XLA Ops:
  7.2 543.7 %all-reduce.3.cloned.1.call-start = ((), (), s32[]{:S(2)}) async-start(), calls=%async_computation | async-start | bytes 62914560 | tf_op jit(solution)/shard_map/psum | solution.py:50
  16.8 37.7 %copy-start.7 = (f32[2048]{0:T(1024)}, f32[2048]{0:T(1024)S(1)}, u32[]{:S(2)}) copy-start(f32[2048]{0:T(1024)S(1)} %add_rsqrt_fusion) | copy-start | bytes 24580
  16.8 23.6 %slice-start.2 = ((s8[10485760]{0:T(1024)(128)(4,1)}), s8[2097152]{0:T(1024)(128)(4,1)S(1)}, s32[]{:S(2)}) async-start(s8[10485760]{0:T(1024)(128)(4,1)} %bitcast.76), calls=%async_computation.3 | async-start | bytes 4194304
  23.5 16.9 %slice-start.3 = ((s8[10485760]{0:T(1024)(128)(4,1)}), s8[4194304]{0:T(1024)(128)(4,1)S(1)}, s32[]{:S(2)}) async-start(s8[10485760]{0:T(1024)(128)(4,1)} %bitcast.76), calls=%async_computation.4 | async-start | bytes 8388608
  23.5 16.9 %slice-start.4 = ((s8[10485760]{0:T(1024)(128)(4,1)}), s8[4194304]{0:T(1024)(128)(4,1)S(1)}, s32[]{:S(2)}) async-start(s8[10485760]{0:T(1024)(128)(4,1)} %bitcast.76), calls=%async_computation.5 | async-start | bytes 8388608
  23.5 16.9 %copy-start.4 = (bf16[1,2048,1024]{2,1,0:T(8,128)(2,1)S(1)}, bf16[1,2048,1024]{2,1,0:T(8,128)(2,1)}, u32[]{:S(2)}) copy-start(bf16[1,2048,1024]{2,1,0:T(8,128)(2,1)} %param.11) | copy-start | bytes 12582916
  54.6 26.7 %copy-start.2 = (bf16[1,2048,1024]{1,2,0:T(8,128)(2,1)S(1)}, bf16[1,2048,1024]{1,2,0:T(8,128)(2,1)}, u32[]{:S(2)}) copy-start(bf16[1,2048,1024]{1,2,0:T(8,128)(2,1)} %copy.20) | copy-start | bytes 12582916
  98.9 18.5 %copy-start.5 = (f32[2048]{0:T(1024)}, f32[2048]{0:T(1024)S(1)}, u32[]{:S(2)}) copy-start(f32[2048]{0:T(1024)S(1)} %get-tuple-element.26) | copy-start | bytes 24580
  211.9 16.6 %copy-start.3 = (bf16[2048,1024]{0,1:T(8,128)(2,1)S(1)}, bf16[2048,1024]{0,1:T(8,128)(2,1)}, u32[]{:S(2)}) copy-start(bf16[2048,1024]{0,1:T(8,128)(2,1)} %get-tuple-element.27) | copy-start | bytes 12582916
  228.4 16.8 %copy-start.6 = (f32[2048]{0:T(1024)S(1)}, f32[2048]{0:T(1024)}, u32[]{:S(2)}) copy-start(f32[2048]{0:T(1024)} %copy-done.5) | copy-start | bytes 24580
  228.4 16.9 %copy-start.1 = (bf16[1,2048,1024]{1,2,0:T(8,128)(2,1)S(1)}, bf16[1,2048,1024]{1,2,0:T(8,128)(2,1)}, u32[]{:S(2)}) copy-start(bf16[1,2048,1024]{1,2,0:T(8,128)(2,1)} %copy.21) | copy-start | bytes 12582916
  264.3 15.6 %copy-start.8 = (f32[2048]{0:T(1024)S(1)}, f32[2048]{0:T(1024)}, u32[]{:S(2)}) copy-start(f32[2048]{0:T(1024)} %copy-done.7) | copy-start | bytes 24580
  550.9 9.5 %slice-start = ((s8[5242880]{0:T(1024)(128)(4,1)}), s8[4194304]{0:T(1024)(128)(4,1)S(1)}, s32[]{:S(2)}) async-start(s8[5242880]{0:T(1024)(128)(4,1)} %bitcast.74), calls=%async_computation.1 | async-start | bytes 8388608
  550.9 9.5 %copy-start = (bf16[1,1024,2560]{2,1,0:T(8,128)(2,1)S(1)}, bf16[1,1024,2560]{2,1,0:T(8,128)(2,1)}, u32[]{:S(2)}) copy-start(bf16[1,1024,2560]{2,1,0:T(8,128)(2,1)} %get-tuple-element.12) | copy-start | bytes 15728644
  550.9 9.5 %slice-start.1 = ((s8[5242880]{0:T(1024)(128)(4,1)}), s8[1048576]{0:T(1024)(128)(4,1)S(1)}, s32[]{:S(2)}) async-start(s8[5242880]{0:T(1024)(128)(4,1)} %bitcast.74), calls=%async_computation.2 | async-start | bytes 2097152
Sparse Core Ops, SparseCore 0:
  325.1 225.7 all-reduce.2
where the time goes:
time: 706 us; the launch traced here: 697 us
  matrix products  298 us (42%)
  waiting for transfers between devices  226 us (32%)
  other arithmetic  143 us (20%)
  between operations  16.6 us (2%)
  local copies, waits for them, and re-layouts  13.2 us (2%)
    psum x1, waiting for transfers between devices, step(): summed[number] = [lax.psum(by_w[name], 'dp') for name in NAMES]  226 us
    convert_element_type x2, other arithmetic, adamw(): return ((w - 0.02 * step).astype(jnp.bfloat16), m, v)  113 us
    dot_general x5, matrix products, layer(): up = jnp.dot(a, w['w_up'], preferred_element_type=jnp.float32)  105 us
    dot_general x5, matrix products, layer(): gate = jnp.dot(a, w['w_gate'], preferred_element_type=jnp.float32)  105 us
    dot_general x5, matrix products, matmul(): jnp.dot(a, w, preferred_element_type=jnp.float32).astype(jnp.bfloat16)  88.1 us
    reduce_sum x3, other arithmetic, step(): jnp.sum(g * g)  24 us
  transfers between devices with their start and end apart: 1, of which 1 were waited for; matrix products, arithmetic and copies ran while one was open for 0% of the time, Pallas kernels for 0%

commit v1 on v0

v1 whole, which is shorter than its diff:
```python
import functools
import math

import jax
import jax.numpy as jnp
from jax import lax
from jax.experimental import pallas as pl
from jax.experimental.pallas import tpu as pltpu
from jax.sharding import PartitionSpec as P

F32, BF16 = jnp.float32, jnp.bfloat16
MESH = pl.DeviceIdType.MESH
VLIM = 64 * 1024 * 1024 - 64 * 1024
DMA = pltpu.SemaphoreType.DMA
ONE = dict(pipeline_mode=pl.Buffered(1))


def dot(a, b):
    return jnp.dot(a, b, preferred_element_type=F32)


def dot_t(a, b):
    return lax.dot_general(a, b, (((1,), (1,)), ((), ())), preferred_element_type=F32)


def t_dot(a, b):
    return lax.dot_general(a, b, (((0,), (0,)), ((), ())), preferred_element_type=F32)


def ds(i, size):
    return pl.ds(pl.multiple_of(i * size, size), size)


def norm_rows(h):
    wide = h.astype(F32)
    scale = lax.rsqrt(jnp.mean(wide * wide, -1, keepdims=True) + 1e-6)
    return (wide * scale).astype(BF16)


class Place:
    def __init__(self, side):
        me = lax.axis_index("dp")
        self.core, chip = lax.rem(me, 2), lax.div(me, 2)
        x, y = lax.div(chip, side), lax.rem(chip, side)
        self.side = side
        at = lambda x, y, core: {"dp": (lax.rem(x + side, side) * side + lax.rem(y + side, side)) * 2 + core}
        self.partner = at(x, y, 1 - self.core)
        along_x = [at(x + k, y, self.core) for k in range(side)]
        along_y = [at(x, y + k, self.core) for k in range(side)]
        self.peers = [self.partner, along_x[1], along_x[-1], along_y[1], along_y[-1]]
        self.rings = [along_x, along_y]
        self.positions = [x, y]
        ring = lambda p, r: (p, r[1], r[-1])
        self.first = [ring(x, along_x), ring(y, along_y)]
        self.second = [ring(y, along_y), ring(x, along_x)]

    def on(self, p, k):
        return lax.rem(p + k, self.side)


def remote(src, dst, send, recv, device):
    return pltpu.make_async_remote_copy(src_ref=src, dst_ref=dst, send_sem=send, recv_sem=recv, device_id=device, device_id_type=MESH)


def greet(peers):
    barrier = pltpu.get_barrier_semaphore()
    for peer in peers:
        pl.semaphore_signal(barrier, inc=1, device_id=peer, device_id_type=MESH)
    pl.semaphore_wait(barrier, len(peers))


def fwd_kernel(x_ref, wg_ref, wu_ref, wd_ref, h_ref, a_ref, gate_ref, up_ref, acc_ref, act_ref, *, mc):
    n, steps = pl.program_id(0), pl.num_programs(0)
    tokens = x_ref.shape[0]
    chunks, block = tokens // mc, tokens // 8

    @pl.when(n == 0)
    def _():
        @pl.loop(0, tokens // block)
        def _(i):
            rows = ds(i, block)
            a_ref[rows, :] = norm_rows(x_ref[rows, :])
            acc_ref[rows, :] = jnp.zeros((block, acc_ref.shape[1]), F32)

    def gu(c):
        rows = pl.ds(c * mc, mc)
        a = a_ref[rows, :]
        gate_ref[0, rows, :] = dot(a, wg_ref[0])
        up_ref[0, rows, :] = dot(a, wu_ref[0])

    def epi(c):
        rows = pl.ds(c * mc, mc)
        g, u = gate_ref[0, rows, :], up_ref[0, rows, :]
        act_ref[rows, :] = (g * jax.nn.sigmoid(g) * u).astype(BF16)

    def down(c):
        rows = pl.ds(c * mc, mc)
        acc_ref[rows, :] += dot(act_ref[rows, :], wd_ref[0])

    gu(0)
    for c in range(chunks):
        if c + 1 < chunks:
            gu(c + 1)
        epi(c)
        if c > 0:
            down(c - 1)
    down(chunks - 1)

    @pl.when(n == steps - 1)
    def _():
        @pl.loop(0, tokens // block)
        def _(i):
            rows = ds(i, block)
            y = acc_ref[rows, :].astype(BF16).astype(F32)
            h_ref[rows, :] = (x_ref[rows, :].astype(F32) + y).astype(BF16)


def fwd(x, wg, wu, wd, layer, tn):
    t, d = x.shape
    ff = wg.shape[2]
    whole = pl.BlockSpec((t, d), lambda n: (0, 0), **ONE)
    tile = pl.BlockSpec((1, t, tn), lambda n: (n, 0, 0))
    return pl.pallas_call(
        functools.partial(fwd_kernel, mc=t // 4),
        grid=(ff // tn,),
        in_specs=[
            whole,
            pl.BlockSpec((1, d, tn), lambda n: (layer, 0, n)),
            pl.BlockSpec((1, d, tn), lambda n: (layer, 0, n)),
            pl.BlockSpec((1, tn, d), lambda n: (layer, n, 0)),
        ],
        out_specs=[whole, whole, tile, tile],
        out_shape=[jax.ShapeDtypeStruct((t, d), BF16)] * 2 + [jax.ShapeDtypeStruct((ff // tn, t, tn), F32)] * 2,
        scratch_shapes=[pltpu.VMEM((t, d), F32), pltpu.VMEM((t, tn), BF16)],
        compiler_params=pltpu.CompilerParams(vmem_limit_bytes=VLIM, dimension_semantics=("arbitrary",)),
        cost_estimate=pl.CostEstimate(flops=6 * t * d * ff, bytes_accessed=10 * t * ff, transcendentals=t * ff),
        name="fwd",
    )(x, wg, wu, wd)


def gates(g, u, dact):
    s = jax.nn.sigmoid(g)
    silu = g * s
    act = (silu * u).astype(BF16)
    dup = (dact * silu).astype(BF16)
    dgate = (dact * u * (s + silu * (1.0 - s))).astype(BF16)
    return act, dgate, dup


DEPTH = 3
RING = 4
STAGES = 11


class Exchange:
    def __init__(self, tiles, place, buffers, semaphores, shard_ref, full_ref, sq_ref):
        self.tiles, self.place = tiles, place
        self.own, self.r0, self.ra, self.rb, self.ra2, self.rb2, self.ta, self.tb, self.ta2, self.tb2, self.total = buffers
        self.sems = semaphores
        self.shard, self.full, self.sq = shard_ref, full_ref, sq_ref
        self.rows = self.r0.shape[2] // place.side
        self.sub = self.rows // place.side

    def pair(self, t, name, axis, src, dst):
        send, recv = self.sems[name]
        slot = lax.rem(t, recv.shape[0])
        copies = []
        for o in range(2):
            for k in range(2):
                copies.append(remote(src(o, k), dst(o, k), send.at[o, k], recv.at[slot, o, k], axis[o][1 + k]))
        return copies

    def d2d(self, t):
        send, recv = self.sems["d2d"]
        slot, core = lax.rem(t, DEPTH), self.place.core
        return [remote(self.own.at[slot, 1 - core], self.r0.at[slot], send, recv.at[slot], self.place.partner)]

    def a(self, t):
        half, slot = self.rows // 2, lax.rem(t, DEPTH)
        return self.pair(t, "a", self.place.first, lambda o, k: self.ta.at[o, pl.ds(k * half, half)], lambda o, k: self.ra.at[slot, o, k])

    def b(self, t):
        slot = lax.rem(t, DEPTH)
        return self.pair(t, "b", self.place.first, lambda o, k: self.tb.at[o, k], lambda o, k: self.rb.at[slot, o, k])

    def a2(self, t):
        half, slot = self.sub // 2, lax.rem(t, DEPTH)
        return self.pair(t, "a2", self.place.second, lambda o, k: self.ta2.at[o, pl.ds(k * half, half)], lambda o, k: self.ra2.at[slot, o, k])

    def b2(self, t):
        slot = lax.rem(t, DEPTH)
        return self.pair(t, "b2", self.place.second, lambda o, k: self.tb2.at[o, k], lambda o, k: self.rb2.at[slot, o, k])

    def cell(self, t, o, step):
        p, q = self.place.first[o][0], self.place.second[o][0]
        return self.full.at[t, self.place.core, o, p * self.place.side + self.place.on(q, step)]

    def keep(self, t):
        slot = lax.rem(t, 2)
        return [pltpu.make_async_copy(self.shard.at[t, o], self.cell(t, o, 0), self.sems["keep"].at[slot, o]) for o in range(2)]

    def d(self, t):
        return self.pair(t, "d", self.place.second, lambda o, k: self.shard.at[t, o], lambda o, k: self.cell(t, o, 0))

    def e(self, t):
        half, side = self.sub // 2, self.place.side
        cut = lambda o, k: self.cell(t, o, (side - 1, 1)[k]).at[pl.ds(k * half, half)]
        return self.pair(t, "e", self.place.second, cut, cut)

    def line(self, t, o, step, first, size):
        i = self.place.on(self.place.first[o][0], step)
        return self.full.at[t, self.place.core, o, pl.ds(i * self.place.side + first, size)]

    def f(self, t):
        cut = lambda o, k: self.line(t, o, 0, 0, self.place.side)
        return self.pair(t, "f", self.place.first, cut, cut)

    def g(self, t):
        side = self.place.side
        cut = lambda o, k: self.line(t, o, (side - 1, 1)[k], k * side // 2, side // 2)
        return self.pair(t, "g", self.place.first, cut, cut)

    def h(self, t):
        send, recv = self.sems["h"]
        half = self.full.at[t, self.place.core]
        return [remote(half, half, send, recv.at[lax.rem(t, RING)], self.place.partner)]

    def chip(self, t, o, first, count):
        at, slot = pl.ds(pl.multiple_of(first, count), count), lax.rem(t, DEPTH)
        return self.own[slot, self.place.core, o, at, :].astype(F32) + self.r0[slot, o, at, :].astype(F32)

    def sum_a(self, t):
        for o in range(2):
            chunk = self.place.on(self.place.first[o][0], 2)
            for i in range(0, self.rows, self.sub):
                self.ta[o, i:i + self.sub, :] = self.chip(t, o, chunk * self.rows + i, self.sub).astype(BF16)

    def sum_b(self, t):
        slot, half, side = lax.rem(t, DEPTH), self.rows // 2, self.place.side
        for o in range(2):
            for k in range(2):
                chunk = self.place.on(self.place.first[o][0], (1, side - 1)[k])
                for i in range(0, self.rows, self.sub):
                    x = self.chip(t, o, chunk * self.rows + i, self.sub)
                    if i // half == k:
                        x = x + self.ra[slot, o, k, i - k * half:i - k * half + self.sub, :].astype(F32)
                    self.tb[o, k, i:i + self.sub, :] = x.astype(BF16)

    def sum_a2(self, t):
        slot, keep = lax.rem(t, DEPTH), lax.rem(t, 2)
        for o in range(2):
            chunk = self.place.first[o][0]
            for i in range(0, self.rows, self.sub):
                x = self.chip(t, o, chunk * self.rows + i, self.sub)
                for k in range(2):
                    x = x + self.rb[slot, o, k, i:i + self.sub, :].astype(F32)
                self.total[keep, o, i:i + self.sub, :] = x
            self.ta2[o] = self.total[keep, o, ds(self.place.on(self.place.second[o][0], 2), self.sub), :].astype(BF16)

    def sum_b2(self, t):
        slot, keep, half, side = lax.rem(t, DEPTH), lax.rem(t, 2), self.sub // 2, self.place.side
        for o in range(2):
            for k in range(2):
                chunk = self.place.on(self.place.second[o][0], (1, side - 1)[k])
                for i in range(2):
                    x = self.total[keep, o, pl.ds(pl.multiple_of(chunk * self.sub + i * half, half), half), :]
                    if i == k:
                        x = x + self.ra2[slot, o, k].astype(F32)
                    self.tb2[o, k, i * half:(i + 1) * half, :] = x.astype(BF16)

    def finish(self, t):
        slot, keep = lax.rem(t, DEPTH), lax.rem(t, 2)
        for o in range(2):
            x = self.total[keep, o, ds(self.place.second[o][0], self.sub), :]
            for k in range(2):
                x = x + self.rb2[slot, o, k].astype(F32)
            g = x.astype(BF16)
            self.shard[t, o] = g
            g = g.astype(F32)
            self.sq[...] += g * g
        for copy in self.keep(t):
            copy.start()

    def kept(self, t):
        for copy in self.keep(t):
            copy.wait()

    def left(self, t):
        @pl.when(t == self.tiles - 1)
        def _():
            for copy in self.h(t):
                copy.wait_send()

    def stage(self, n, k, start, before=None, work=None):
        t = n - k
        if start is not None:
            @pl.when((t >= 1) & (t <= self.tiles))
            def _():
                for copy in start(t - 1):
                    copy.wait_send()

        @pl.when((t >= 0) & (t < self.tiles))
        def _():
            if before is not None:
                for copy in before(t):
                    copy.wait_recv()
            if work is not None:
                work(t)
            if start is not None:
                for copy in start(t):
                    copy.start()

    def inside(self, n):
        self.stage(n, 1, self.a, self.d2d, self.sum_a)
        self.stage(n, 2, self.a2, self.b, self.sum_a2)
        self.stage(n, 3, self.d, self.b2, self.finish)
        self.stage(n, 4, self.f, self.e, self.kept)
        self.stage(n, 5, self.h, self.g)

    def after(self, n):
        self.stage(n, 0, self.d2d)
        self.stage(n, 1, self.b, self.a, self.sum_b)
        self.stage(n, 2, self.b2, self.a2, self.sum_b2)
        self.stage(n, 3, self.e, self.d)
        self.stage(n, 4, self.g, self.f)
        self.stage(n, 5, None, self.h, self.left)


class Total:
    def __init__(self, place, sums, send, recv):
        self.place, self.sums, self.send, self.recv = place, sums, send, recv
        self.members = [[None, place.partner], *place.rings]
        self.me = [place.core, *place.positions]

    def copies(self, k):
        here = self.sums.at[k, self.me[k]]
        return [remote(here, here, self.send.at[k, i], self.recv.at[k, i], peer) for i, peer in enumerate(self.members[k]) if i]

    def start(self, k, value):
        self.sums[k, self.me[k]] = value
        for copy in self.copies(k):
            copy.start()

    def end(self, k):
        for copy in self.copies(k):
            copy.wait()
        value = self.sums[k, 0]
        for i in range(1, len(self.members[k])):
            value = value + self.sums[k, i]
        return value


def grads_kernel(h_ref, dy_ref, wg_ref, wu_ref, wd_ref, a0_hbm, gate_hbm, up_hbm, full_ref, factor_ref,
                 a_ref, a0_ref, da_ref, g_ref, u_ref, dact_ref, act_ref, dgu_ref,
                 own, r0, ra, rb, ra2, rb2, ta, tb, ta2, tb2, total, shard_ref, sq_ref, sums,
                 a0_sem, gu_sem, vs, vr, keep_sem, s0, q0, sh, qh, *pairs, mc, side, tiles, count):
    n = pl.program_id(0)
    tokens, d = h_ref.shape
    tn = wg_ref.shape[2]
    chunks, block = tokens // mc, tokens // 8
    place = Place(side)
    piece = d // (2 * side * side)
    sems = {name: pairs[2 * i:2 * i + 2] for i, name in enumerate(("a", "b", "a2", "b2", "d", "e", "f", "g"))}
    sems.update(d2d=(s0, q0), h=(sh, qh), keep=keep_sem)
    exchange = Exchange(
        2 * tiles, place, (own, r0, ra, rb, ra2, rb2, ta, tb, ta2, tb2, total), sems, shard_ref, full_ref, sq_ref
    )
    squares = Total(place, sums, vs, vr)

    def load_a0():
        return pltpu.make_async_copy(a0_hbm, a0_ref, a0_sem)

    def load_gu(t):
        slot = lax.rem(t + 1, 2)
        return (
            pltpu.make_async_copy(gate_hbm.at[t], g_ref.at[slot], gu_sem.at[slot, 0]),
            pltpu.make_async_copy(up_hbm.at[t], u_ref.at[slot], gu_sem.at[slot, 1]),
        )

    @pl.when(n == 0)
    def _():
        load_a0().start()
        greet([place.partner, *place.rings[0][1:], *place.rings[1][1:]])
        sq_ref[...] = jnp.zeros_like(sq_ref)

        @pl.loop(0, tokens // block)
        def _(i):
            rows = ds(i, block)
            a_ref[rows, :] = norm_rows(h_ref[rows, :])
            da_ref[rows, :] = jnp.zeros((block, d), F32)

    @pl.when((n >= tiles - 1) & (n < 2 * tiles - 1))
    def _():
        for copy in load_gu(n + 1 - tiles):
            copy.start()

    def weights_down(act, right):
        slot = lax.rem(n, DEPTH)
        down = t_dot(act[...], right[...]).astype(BF16)
        lanes = d // (2 * side)
        for o in range(2):
            for c in range(2):
                for i in range(side):
                    for j in range(side):
                        k = (i * side + j) * piece
                        own[slot, c, o, k:k + piece, tn:] = down[
                            (o * side + i) * piece:(o * side + i + 1) * piece, (c * side + j) * lanes:(c * side + j + 1) * lanes
                        ]

    def weights_in(left, dgu):
        slot, half = lax.rem(n, DEPTH), d // 2
        for c in range(2):
            at = left[:, c * half:(c + 1) * half]
            own[slot, c, 0, :, :tn] = t_dot(at, dgu[:, :tn]).astype(BF16)
            own[slot, c, 1, :, :tn] = t_dot(at, dgu[:, tn:]).astype(BF16)

    def epi(c, g, u):
        rows = pl.ds(c * mc, mc)
        dact = dact_ref[rows, :].astype(BF16).astype(F32)
        act, dgate, dup = gates(g[rows, :], u[rows, :], dact)
        act_ref[rows, :] = act
        dgu_ref[rows, :tn] = dgate
        dgu_ref[rows, tn:] = dup

    last, first = n < tiles, (n >= tiles) & (n < 2 * tiles)

    @pl.when(last)
    def _():
        def gud(c):
            rows = pl.ds(c * mc, mc)
            a = a_ref[rows, :]
            g_ref[0, rows, :] = dot(a, wg_ref[0])
            u_ref[0, rows, :] = dot(a, wu_ref[0])
            dact_ref[rows, :] = dot_t(dy_ref[rows, :], wd_ref[0])

        def back(c):
            rows = pl.ds(c * mc, mc)
            da_ref[rows, :] += dot_t(dgu_ref[rows, :tn], wg_ref[0]) + dot_t(dgu_ref[rows, tn:], wu_ref[0])

        gud(0)
        for c in range(1, chunks):
            gud(c)
            epi(c - 1, g_ref.at[0], u_ref.at[0])
        for c in range(chunks - 1):
            back(c)
            if c == 0:
                epi(chunks - 1, g_ref.at[0], u_ref.at[0])
        back(chunks - 1)

    @pl.when(first)
    def _():
        t = n - tiles
        slot = lax.rem(t + 1, 2)
        for copy in load_gu(t):
            copy.wait()

        def da(c):
            rows = pl.ds(c * mc, mc)
            dact_ref[rows, :] = dot_t(a_ref[rows, :], wd_ref[0])

        da(0)
        for c in range(1, chunks):
            da(c)
            epi(c - 1, g_ref.at[slot], u_ref.at[slot])
        epi(chunks - 1, g_ref.at[slot], u_ref.at[slot])
        weights_down(act_ref, a_ref)

    exchange.inside(n)

    @pl.when(n == 2 * tiles + 2)
    def _():
        squares.start(0, jnp.full(factor_ref.shape, jnp.sum(sq_ref[...]), F32))

    @pl.when(n == 2 * tiles + 3)
    def _():
        squares.start(2, squares.end(1))

    @pl.when(last)
    def _():
        weights_down(act_ref, dy_ref)
        weights_in(a_ref, dgu_ref)

    @pl.when(first)
    def _():
        weights_in(a0_ref, dgu_ref)

    exchange.after(n)

    @pl.when(n == tiles - 1)
    def _():
        @pl.loop(0, tokens // block)
        def _(i):
            rows = ds(i, block)
            da = da_ref[rows, :].astype(BF16).astype(F32)
            h = h_ref[rows, :].astype(F32)
            ms = jnp.mean(h * h, -1, keepdims=True) + 1e-6
            r = lax.rsqrt(ms)
            along = jnp.mean(da * h, -1, keepdims=True)
            dn = (r * (da - h * (along / ms))).astype(BF16).astype(F32)
            a_ref[rows, :] = (dy_ref[rows, :].astype(F32) + dn).astype(BF16)

        load_a0().wait()

    @pl.when(n == 2 * tiles + 2)
    def _():
        squares.start(1, squares.end(0))

    @pl.when(n == 2 * tiles + 3)
    def _():
        factor_ref[...] = jnp.minimum(1.0, 0.5 * lax.rsqrt(squares.end(2) / count + 1e-30))


def grads(h, dy, wg, wu, wd, a0, gate, up, tn, side, count):
    t, d = h.shape
    ff = wg.shape[2]
    tiles = ff // tn
    piece, wide = d // (2 * side * side), tn + d // (2 * side)
    chunk = side * piece
    rows = side * chunk
    whole = pl.BlockSpec((t, d), lambda n: (0, 0), **ONE)
    hbm = pl.BlockSpec(memory_space=pl.ANY)
    mid = lambda n: jnp.minimum(n, tiles - 1)
    full = (2 * tiles, 2, 2, side * side, piece, wide)
    return pl.pallas_call(
        functools.partial(grads_kernel, mc=t // 4, side=side, tiles=tiles, count=count),
        grid=(2 * tiles + 5,),
        in_specs=[
            whole,
            whole,
            pl.BlockSpec((1, d, tn), lambda n: (1, 0, mid(n))),
            pl.BlockSpec((1, d, tn), lambda n: (1, 0, mid(n))),
            pl.BlockSpec((1, tn, d), lambda n: (jnp.where(n < tiles, 1, 0), jnp.where(n < tiles, n, jnp.minimum(n - tiles, tiles - 1)), 0)),
            hbm,
            hbm,
            hbm,
        ],
        out_specs=[hbm, pl.BlockSpec((8, 128), lambda n: (0, 0), **ONE)],
        out_shape=[jax.ShapeDtypeStruct(full, BF16), jax.ShapeDtypeStruct((8, 128), F32)],
        scratch_shapes=[
            pltpu.VMEM((t, d), BF16), pltpu.VMEM((t, d), BF16), pltpu.VMEM((t, d), F32),
            pltpu.VMEM((2, t, tn), F32), pltpu.VMEM((2, t, tn), F32), pltpu.VMEM((t, tn), F32),
            pltpu.VMEM((t, tn), BF16), pltpu.VMEM((t, 2 * tn), BF16),
            pltpu.VMEM((DEPTH, 2, 2, rows, wide), BF16),
            pltpu.VMEM((DEPTH, 2, rows, wide), BF16),
            pltpu.VMEM((DEPTH, 2, 2, chunk // 2, wide), BF16),
            pltpu.VMEM((DEPTH, 2, 2, chunk, wide), BF16),
            pltpu.VMEM((DEPTH, 2, 2, piece // 2, wide), BF16),
            pltpu.VMEM((DEPTH, 2, 2, piece, wide), BF16),
            pltpu.VMEM((2, chunk, wide), BF16),
            pltpu.VMEM((2, 2, chunk, wide), BF16),
            pltpu.VMEM((2, piece, wide), BF16),
            pltpu.VMEM((2, 2, piece, wide), BF16),
            pltpu.VMEM((2, 2, chunk, wide), F32),
            pltpu.VMEM((2 * tiles, 2, piece, wide), BF16),
            pltpu.VMEM((piece, wide), F32),
            pltpu.VMEM((3, side, 8, 128), F32),
            DMA, DMA((2, 2)), DMA((3, side)), DMA((3, side)), DMA((2, 2)),
            DMA, DMA((DEPTH,)), DMA, DMA((RING,)),
            *[sem for name in range(4) for sem in (DMA((2, 2)), DMA((DEPTH, 2, 2)))],
            *[sem for name in range(4) for sem in (DMA((2, 2)), DMA((RING, 2, 2)))],
        ],
        compiler_params=pltpu.CompilerParams(
            vmem_limit_bytes=VLIM, dimension_semantics=("arbitrary",), collective_id=0, has_side_effects=True
        ),
        cost_estimate=pl.CostEstimate(flops=24 * t * d * ff, bytes_accessed=20 * d * ff, transcendentals=2 * t * ff),
        name="grads",
    )(h, dy, wg, wu, wd, a0, gate, up)


def adam_kernel(factor_ref, full_ref, *refs, side):
    weights, moments, squares, new_w, new_m, new_v = (refs[i:i + 3] for i in range(0, 18, 3))
    part = pl.program_id(1)
    piece, wide = full_ref.shape[4:]
    tn = new_w[0].shape[2]
    lanes = wide - tn
    f = factor_ref[0, 0]

    def step(k, at, g):
        g = g.astype(F32) * f
        m = 0.9 * moments[k][at] + 0.1 * g
        v = 0.95 * squares[k][at] + 0.05 * (g * g)
        w = weights[k][at].astype(F32)
        new_w[k][at] = (w - 0.02 * (m * lax.rsqrt(v + 1e-8) + 0.1 * w)).astype(BF16)
        new_m[k][at] = m
        new_v[k][at] = v

    @pl.loop(0, side)
    def _(i):
        for j in range(side):
            rows = ds(i * side + j, piece)
            for o in range(2):
                step(o, (0, rows, slice(None)), full_ref[0, part, o, i * side + j, :, :tn])
        rows = ds(i, piece)
        for c in range(2):
            for j in range(side):
                at = (0, rows, slice((c * side + j) * lanes, (c * side + j + 1) * lanes))
                step(2, at, full_ref[0, c, part, i * side + j, :, tn:])


def adam(factor, full, ws, ms, vs, tn, side):
    _, d, ff = ws[0].shape
    tiles = ff // tn
    layer = lambda t: 1 - t // tiles
    up = pl.BlockSpec((1, d // 2, tn), lambda t, c: (layer(t), c, t % tiles))
    down = pl.BlockSpec((1, tn // 2, d), lambda t, c: (layer(t), (t % tiles) * 2 + c, 0))
    blocks = [up, up, down]
    size = sum(w.size for w in ws)
    out = pl.pallas_call(
        functools.partial(adam_kernel, side=side),
        grid=(2 * tiles, 2),
        in_specs=[
            pl.BlockSpec(factor.shape, lambda t, c: (0, 0), **ONE),
            pl.BlockSpec((1, *full.shape[1:]), lambda t, c: (t, 0, 0, 0, 0, 0)),
            *blocks * 3,
        ],
        out_specs=blocks * 3,
        out_shape=[jax.ShapeDtypeStruct(a.shape, a.dtype) for a in (*ws, *ms, *vs)],
        compiler_params=pltpu.CompilerParams(vmem_limit_bytes=VLIM, dimension_semantics=("arbitrary", "arbitrary")),
        cost_estimate=pl.CostEstimate(flops=20 * size, bytes_accessed=22 * size, transcendentals=size),
        name="adam",
    )(factor, full, *ws, *ms, *vs)
    return tuple(out)


def solution(mesh):
    side = math.isqrt(mesh.shape["dp"] // 2)

    def step(x, dy, *arrays):
        ws, ms, vs = (arrays[i:i + 3] for i in (0, 3, 6))
        wg, wu, wd = ws
        x, dy = x[0], dy[0]
        tn = x.shape[1] // side
        h, a0, gate, up = fwd(x, wg, wu, wd, 0, tn)
        full, factor = grads(h, dy, wg, wu, wd, a0, gate, up, tn, side, sum(w.size for w in ws))
        return adam(factor, full, ws, ms, vs, tn, side)

    return jax.shard_map(
        step,
        mesh=mesh,
        in_specs=(P(("rep", "dp"), None, None),) * 2 + (P(None, None, None),) * 9,
        out_specs=(P("rep", None, None),) * 9,
        check_vma=False,
    )
```

time: 706 us -> 437 us (0.62); the launches traced: 697 us -> 437 us
  Pallas kernels: 0 us -> 436 us
  matrix products: 298 us -> 0 us
  waiting for transfers between devices: 226 us -> 0 us
  other arithmetic: 143 us -> 0 us
  between operations: 16.6 us -> 0.81 us
  local copies, waits for them, and re-layouts: 13.2 us -> 0 us
    pallas_call x0 -> x3, Pallas kernels: none -> 436 us  [the longest x1 263 us: grads(): pl.pallas_call(functools.partial(grads_kernel, mc=t // 4, side=side, tile...]
    dot_general x15 -> x0, matrix products: 298 us -> none  [the longest x5 105 us: layer(): up = jnp.dot(a, w['w_up'], preferred_element_type=jnp.float32)]
    psum x1 -> x0, waiting for transfers between devices: 226 us -> none  [step(): summed[number] = [lax.psum(by_w[name], 'dp') for name in NAMES]]
    convert_element_type x2 -> x0, other arithmetic: 113 us -> none  [adamw(): return ((w - 0.02 * step).astype(jnp.bfloat16), m, v)]
    reduce_sum x4 -> x0, other arithmetic: 27 us -> none  [the longest x3 24 us: step(): jnp.sum(g * g)]
    unnamed x30 -> x0, local copies, waits for them, and re-layouts: 13.2 us -> none
  transfers between devices with their start and end apart: 1 -> 0, of which waited for: 1 -> 0; matrix products, arithmetic and copies ran while one was open for 0% -> 0% of each run, Pallas kernels for 0% -> 0%
where the time goes in v1:
time: 437 us
  Pallas kernels  436 us (100%)
    pallas_call x1, Pallas kernels, grads(): pl.pallas_call(functools.partial(grads_kernel, mc=t // 4, side=side, tile...  263 us
    pallas_call x1, Pallas kernels, adam(): pl.pallas_call(functools.partial(adam_kernel, side=side), grid=(2 * tiles...  127 us
    pallas_call x1, Pallas kernels, fwd(): pl.pallas_call(functools.partial(fwd_kernel, mc=t // 4), grid=(ff // tn,)...  45.5 us

profile of v1, /device:TPU:97, one launch (start us, length us, event | category | flops | bytes accessed | tf_op | source)
XLA Modules:
  0.0 437.1 jit_solution(200869648751932033)
XLA Ops:
  0.6 45.5 %fwd.1 = (bf16[2048,1024]{1,0:T(8,128)(2,1)}, bf16[2048,1024]{1,0:T(8,128)(2,1)}, f32[10,2048,256]{2,1,0:T(8,128)}, f32[10,2048,256]{2,1,0:T(8,128)}) custom-call(bf16[2048,1024]{1,0:T(8,128)(2,1)} %bitcast.2, bf16[2,1024,2560]{2,1,0:T(8,128)(2,1)} %refs_0_.1, bf16[2,1024,2560]{2,1,0:T(8,128)(2,1)} %refs_1_.1, bf16[2,2560,1024]{2,1,0:T(8,128)(2,1)} %refs_2_.1), custom_call_target="tpu_custom_call" | custom-call | flops 32212254720 | bytes 52428800 | tf_op jit(solution)/shard_map/fwd/pallas_call | solution.py:123
  46.2 263.4 %grads.1 = (bf16[20,2,2,16,32,384]{5,4,3,2,1,0:T(8,128)(2,1)}, f32[8,128]{1,0:T(8,128)}) custom-call(bf16[2048,1024]{1,0:T(8,128)(2,1)} %get-tuple-element.15.h_ref, bf16[2048,1024]{1,0:T(8,128)(2,1)} %bitcast.3, bf16[2,1024,2560]{2,1,0:T(8,128)(2,1)} %refs_0_.1, bf16[2,1024,2560]{2,1,0:T(8,128)(2,1)} %refs_1_.1, bf16[2,2560,1024]{2,1,0:T(8,128)(2,1)} %refs_2_.1, ...), custom_call_target="tpu_custom_call" | custom-call | flops 128849018880 | bytes 52428800 | tf_op jit(solution)/shard_map/grads/pallas_call | solution.py:524
  309.6 127.4 %adam.1 = (bf16[2,1024,2560]{2,1,0:T(8,128)(2,1)}, bf16[2,1024,2560]{2,1,0:T(8,128)(2,1)}, bf16[2,2560,1024]{2,1,0:T(8,128)(2,1)}, f32[2,1024,2560]{2,1,0:T(8,12...) custom-call(f32[8,128]{1,0:T(8,128)} %get-tuple-element.19.factor_re, ...), custom_call_target="tpu_custom_call" | custom-call | flops 314572800 | bytes 346030080 | tf_op jit(solution)/shard_map/adam/pallas_call | solution.py:608

commit v2 on v0

v2 whole, which is shorter than its diff:
```python
import functools
import math

import jax
import jax.numpy as jnp
from jax import lax
from jax.experimental import pallas as pl
from jax.experimental.pallas import tpu as pltpu
from jax.sharding import PartitionSpec as P

F32, BF16 = jnp.float32, jnp.bfloat16
MESH = pl.DeviceIdType.MESH
VLIM = 64 * 1024 * 1024 - 64 * 1024
DMA = pltpu.SemaphoreType.DMA
ONE = dict(pipeline_mode=pl.Buffered(1))


def dot(a, b):
    return jnp.dot(a, b, preferred_element_type=F32)


def dot_t(a, b):
    return lax.dot_general(a, b, (((1,), (1,)), ((), ())), preferred_element_type=F32)


def t_dot(a, b):
    return lax.dot_general(a, b, (((0,), (0,)), ((), ())), preferred_element_type=F32)


def ds(i, size):
    return pl.ds(pl.multiple_of(i * size, size), size)


def norm_rows(h):
    wide = h.astype(F32)
    scale = lax.rsqrt(jnp.mean(wide * wide, -1, keepdims=True) + 1e-6)
    return (wide * scale).astype(BF16)


class Place:
    def __init__(self, side):
        me = lax.axis_index("dp")
        self.core, chip = lax.rem(me, 2), lax.div(me, 2)
        x, y = lax.div(chip, side), lax.rem(chip, side)
        self.side = side
        at = lambda x, y, core: {"dp": (lax.rem(x + side, side) * side + lax.rem(y + side, side)) * 2 + core}
        self.partner = at(x, y, 1 - self.core)
        along_x = [at(x + k, y, self.core) for k in range(side)]
        along_y = [at(x, y + k, self.core) for k in range(side)]
        self.peers = [self.partner, along_x[1], along_x[-1], along_y[1], along_y[-1]]
        self.rings = [along_x, along_y]
        self.positions = [x * 2 + self.core, y]
        self.members = [[at(x + r // 2, y, lax.rem(self.core + r % 2, 2)) for r in range(2 * side)], along_y]
        ring = lambda p, r: (p, r[1], r[-1])
        self.first = [ring(x, along_x), ring(y, along_y)]
        self.second = [ring(y, along_y), ring(x, along_x)]

    def on(self, p, k):
        return lax.rem(p + k, self.side)


def remote(src, dst, send, recv, device):
    return pltpu.make_async_remote_copy(src_ref=src, dst_ref=dst, send_sem=send, recv_sem=recv, device_id=device, device_id_type=MESH)


def greet(peers):
    barrier = pltpu.get_barrier_semaphore()
    for peer in peers:
        pl.semaphore_signal(barrier, inc=1, device_id=peer, device_id_type=MESH)
    pl.semaphore_wait(barrier, len(peers))


OWN = 4
MATE = 4
DEPTH = 2
GROUP = 2
FINISH = 5


class Exchange:
    def __init__(self, tiles, gathered, place, buffers, semaphores, shard_ref, full_ref, rest_ref, sq_ref):
        self.tiles, self.gathered, self.place = tiles, gathered, place
        self.early = tiles // 2
        self.own, self.mate, self.out, self.inn, self.total = buffers
        self.sems = semaphores
        self.shard, self.full, self.rest, self.sq = shard_ref, full_ref, rest_ref, sq_ref
        self.rows = self.mate.shape[2] // place.side
        self.sub = self.rows // place.side
        half, small = self.rows // 2, self.sub // 2
        self.a, self.a2, self.b2, self.b = 0, half, half + small, half + small + self.sub

    def tile(self, tick):
        two = tick < 2 * self.early
        there = (tick >= 0) & (tick < self.tiles + self.early) & ((lax.rem(tick + 4 * self.tiles, 2) == 1) | jnp.logical_not(two))
        return jnp.where(two, lax.div(tick, 2), tick - self.early), there

    def neighbours(self):
        return [(axis, k, self.place.first[axis][1 + k]) for axis in range(2) for k in range(2)]

    def ring(self, tick, first, stop):
        slot = lax.rem(tick, DEPTH)
        send, recv = self.sems["ring"]
        rows = pl.ds(first, stop - first)
        return [
            remote(self.out.at[i, k, rows], self.inn.at[slot, i, k, rows], send, recv.at[slot], peer) for i, k, peer in self.neighbours()
        ]

    def ring_all(self, tick, first, stop, which):
        slot = lax.rem(tick, DEPTH)
        ref = self.inn.at[slot, :, :, pl.ds(first, stop - first)]
        send, recv = self.sems["ring"]
        return pltpu.make_async_copy(ref, ref, send if which == 0 else recv.at[slot])

    def in_parts(self, tick, what):
        end, middle, last = self.b + self.rows, 2 * self.early, self.tiles + self.early
        odd = lax.rem(tick + 2, 2) == 1
        for when, first, stop in (
            ((tick >= 0) & (tick < middle) & jnp.logical_not(odd), self.a, self.b2),
            ((tick >= 0) & (tick < middle) & odd, self.b2, end),
            ((tick >= middle) & (tick <= last), self.a, end),
            (tick == last + 1, self.a2, end),
            (tick == last + 2, self.a2, self.b),
            (tick == last + 3, self.b2, self.b),
        ):
            pl.when(when)(functools.partial(what, first, stop))

    def d2d(self, t):
        send, recv = self.sems["d2d"]
        two, mate = lax.rem(t, 2), lax.rem(t, MATE)
        return remote(self.own.at[OWN + two], self.mate.at[mate], send.at[two], recv.at[mate], self.place.partner)

    def chip(self, t, o, first, count):
        at = pl.ds(pl.multiple_of(first, count), count)
        return self.own[lax.rem(t, OWN), o, at, :].astype(F32) + self.mate[lax.rem(t, MATE), o, at, :].astype(F32)

    def sum_a(self, t, slot):
        half = self.rows // 2
        for o in range(2):
            chunk = self.place.on(self.place.first[o][0], 2)
            for i in range(0, self.rows, self.sub):
                at = self.a + i % half
                self.out[o, i // half, at:at + self.sub, :] = self.chip(t, o, chunk * self.rows + i, self.sub).astype(BF16)

    def sum_b(self, t, slot, k):
        half, side = self.rows // 2, self.place.side
        for o in range(2):
            chunk = self.place.on(self.place.first[o][0], (1, side - 1)[k])
            for i in range(0, self.rows, self.sub):
                x = self.chip(t, o, chunk * self.rows + i, self.sub)
                if i // half == k:
                    at = self.a + i % half
                    x = x + self.inn[slot, o, k, at:at + self.sub, :].astype(F32)
                at = self.b + i
                self.out[o, k, at:at + self.sub, :] = x.astype(BF16)

    def sum_a2(self, t, slot, o):
        keep, half = lax.rem(t, DEPTH), self.sub // 2
        chunk = self.place.first[o][0]
        for i in range(0, self.rows, self.sub):
            x = self.chip(t, o, chunk * self.rows + i, self.sub)
            at = self.b + i
            for k in range(2):
                x = x + self.inn[slot, o, k, at:at + self.sub, :].astype(F32)
            self.total[keep, o, i:i + self.sub, :] = x
        far = self.place.on(self.place.second[o][0], 2)
        for k in range(2):
            x = self.total[keep, o, pl.ds(pl.multiple_of(far * self.sub + k * half, half), half), :]
            self.out[1 - o, k, self.a2:self.a2 + half, :] = x.astype(BF16)

    def sum_b2(self, t, slot):
        keep, half, side = lax.rem(t, DEPTH), self.sub // 2, self.place.side
        for o in range(2):
            for k in range(2):
                chunk = self.place.on(self.place.second[o][0], (1, side - 1)[k])
                for i in range(2):
                    x = self.total[keep, o, pl.ds(pl.multiple_of(chunk * self.sub + i * half, half), half), :]
                    if i == k:
                        x = x + self.inn[slot, 1 - o, k, self.a2:self.a2 + half, :].astype(F32)
                    at = self.b2 + i * half
                    self.out[1 - o, k, at:at + half, :] = x.astype(BF16)

    def finish(self, t, slot):
        keep = lax.rem(t, DEPTH)
        for o in range(2):
            x = self.total[keep, o, ds(self.place.second[o][0], self.sub), :]
            for k in range(2):
                x = x + self.inn[slot, 1 - o, k, self.b2:self.b2 + self.sub, :].astype(F32)
            g = x.astype(BF16)
            self.shard[t, o] = g
            g = g.astype(F32)
            self.sq[...] += g * g

        @pl.when(t >= self.gathered)
        def _():
            self.rest[t - self.gathered] = self.shard[t]

    def tiles_of(self, q):
        return pl.ds(q * GROUP, GROUP)

    def cell(self, q, o, step):
        p, at = self.place.first[o][0], self.place.second[o][0]
        return self.full.at[self.tiles_of(q), self.place.core, o, p * self.place.side + self.place.on(at, step)]

    def line(self, q, o, step, first, size):
        i = self.place.on(self.place.first[o][0], step)
        return self.full.at[self.tiles_of(q), self.place.core, o, pl.ds(i * self.place.side + first, size)]

    def keep(self, q):
        return [
            pltpu.make_async_copy(self.shard.at[self.tiles_of(q), o], self.cell(q, o, 0), self.sems["keep"].at[lax.rem(q, DEPTH), o])
            for o in range(2)
        ]

    def gather(self, name, q):
        send, recv = self.sems[name]
        recv = recv.at[lax.rem(q, DEPTH)]
        side, half = self.place.side, self.sub // 2
        if name == "h":
            both = self.full.at[self.tiles_of(q), self.place.core]
            return [remote(both, both, send, recv, self.place.partner)]
        copies = []
        for o in range(2):
            for k in range(2):
                back = (side - 1, 1)[k]
                if name == "d":
                    src, dst = self.shard.at[self.tiles_of(q), o], self.cell(q, o, 0)
                elif name == "e":
                    p, at = self.place.first[o][0], self.place.second[o][0]
                    src = dst = self.full.at[
                        self.tiles_of(q), self.place.core, o, p * side + self.place.on(at, back), pl.ds(k * half, half)
                    ]
                elif name == "f":
                    src = dst = self.line(q, o, 0, 0, side)
                else:
                    src = dst = self.line(q, o, back, k * side // 2, side // 2)
                axis = self.place.second if name in "de" else self.place.first
                copies.append(remote(src, dst, send, recv, axis[o][1 + k]))
        return copies

    def gather_all(self, name, q, which):
        send, recv = self.sems[name]
        side = self.place.side
        if name == "d":
            ref = self.shard.at[pl.ds(0, 2 * GROUP)]
        elif name == "e":
            ref = self.shard.at[pl.ds(0, GROUP)]
        elif name == "f":
            ref = self.full.at[pl.ds(0, GROUP), 0, 0]
        elif name == "g":
            ref = self.full.at[pl.ds(0, GROUP), 0, 0, pl.ds(0, side * side // 2)]
        else:
            ref = self.full.at[pl.ds(0, GROUP), 0]
        return pltpu.make_async_copy(ref, ref, send if which == 0 else recv.at[lax.rem(q, DEPTH)])

    def gather_step(self, tick, i, before, after):
        t, there = self.tile(tick - FINISH - 1 - i)
        q = lax.div(t, GROUP)

        @pl.when(there & (t < self.gathered) & (lax.rem(t, GROUP) == GROUP - 1))
        def _():
            if before:
                self.gather_all(before, q, 1).wait()
                self.gather_all(before, q, 0).wait()
            if after == "f":
                for copy in self.keep(q):
                    copy.wait()
            if after:
                for copy in self.gather(after, q):
                    copy.start()
            if after == "d":
                for copy in self.keep(q):
                    copy.start()

    def tick(self, tick):
        def ring_wait(first, stop):
            self.ring_all(tick - 1, first, stop, 1).wait()
            self.ring_all(tick - 1, first, stop, 0).wait()

        def ring_start(first, stop):
            for copy in self.ring(tick, first, stop):
                copy.start()

        slot = lax.rem(tick + 1, DEPTH)
        self.in_parts(tick - 1, ring_wait)

        t5, there = self.tile(tick - FINISH)
        pl.when(there)(lambda: self.finish(t5, slot))

        t, there = self.tile(tick - 2)

        @pl.when(there)
        def _():
            self.sum_b(t, slot, 0)
            self.sum_b(t, slot, 1)

        t1, there = self.tile(tick - 1)

        @pl.when(there)
        def _():
            self.d2d(t1).wait_recv()
            self.d2d(t1).wait_send()
            self.sum_a(t1, slot)

        t3, there = self.tile(tick - 3)

        @pl.when(there)
        def _():
            self.sum_a2(t3, slot, 0)
            self.sum_a2(t3, slot, 1)

        t4, there = self.tile(tick - 4)

        @pl.when(there)
        def _():
            self.sum_b2(t4, slot)

        t0, there = self.tile(tick)

        @pl.when(there)
        def _():
            self.d2d(t0).start()

        self.in_parts(tick, ring_start)

        stages = ("d", "e", "f", "g", "h", "")
        for i in reversed(range(6)):
            self.gather_step(tick, i, stages[i - 1] if i else "", stages[i])


class Total:
    def __init__(self, place, sums, send, recv):
        self.place, self.sums, self.send, self.recv = place, sums, send, recv

    def over(self, k, value):
        members, me = self.place.members[k], self.place.positions[k]
        self.sums[k, me] = value
        here = self.sums.at[k, me]
        copies = [remote(here, here, self.send.at[k, i], self.recv.at[k, i], peer) for i, peer in enumerate(members) if i]
        for copy in copies:
            copy.start()
        for copy in copies:
            copy.wait()
        value = self.sums[k, 0]
        for i in range(1, len(members)):
            value = value + self.sums[k, i]
        return value


def gates(g, u, dact):
    s = jax.nn.sigmoid(g)
    silu = g * s
    act = (silu * u).astype(BF16)
    dup = (dact * silu).astype(BF16)
    dgate = (dact * u * (s + silu * (1.0 - s))).astype(BF16)
    return act, dgate, dup


def layers_kernel(x_hbm, dy_hbm, wg_ref, wu_ref, wd_ref, full_ref, rest_ref, factor_ref, gate_hbm, up_hbm,
                  dy_ref, h_ref, a_ref, a0_ref, acc_ref, g_ref, u_ref, dact_ref, act_ref, dgu_ref,
                  own, mate, out, inn, total, shard_ref, sq_ref, sums,
                  x_sem, dy_sem, gu_sem, vs, vr, keep_sem, *pairs, mc, side, tiles, gathered, count):
    step = pl.program_id(0)
    n = step - tiles
    tokens, d = h_ref.shape
    tn = wg_ref.shape[2]
    chunks, blocks = tokens // mc, x_sem.shape[0]
    block = tokens // blocks
    place = Place(side)
    piece = d // (2 * side * side)
    sems = {name: pairs[2 * i:2 * i + 2] for i, name in enumerate(("d2d", "ring", "d", "e", "f", "g", "h"))}
    sems["keep"] = keep_sem
    exchange = Exchange(2 * tiles, gathered, place, (own, mate, out, inn, total), sems, shard_ref, full_ref, rest_ref, sq_ref)

    def load_x(i):
        rows = ds(i, block)
        return pltpu.make_async_copy(x_hbm.at[rows], h_ref.at[rows], x_sem.at[i])

    def load_dy():
        return pltpu.make_async_copy(dy_hbm, dy_ref, dy_sem)

    def put_gu(t):
        slot = lax.rem(t, 2)
        return (
            pltpu.make_async_copy(g_ref.at[slot], gate_hbm.at[t], gu_sem.at[slot, 0]),
            pltpu.make_async_copy(u_ref.at[slot], up_hbm.at[t], gu_sem.at[slot, 1]),
        )

    def get_gu(t):
        slot = lax.rem(t + 1, 2)
        return (
            pltpu.make_async_copy(gate_hbm.at[t], g_ref.at[slot], gu_sem.at[slot, 0]),
            pltpu.make_async_copy(up_hbm.at[t], u_ref.at[slot], gu_sem.at[slot, 1]),
        )

    @pl.when(step == 0)
    def _():
        for i in range(blocks):
            load_x(i).start()
        load_dy().start()
        greet([*place.members[0][1:], *place.members[1][1:]])
        sq_ref[...] = jnp.zeros_like(sq_ref)

        @pl.loop(0, blocks)
        def _(i):
            rows = ds(i, block)
            load_x(i).wait()
            a0_ref[rows, :] = norm_rows(h_ref[rows, :])
            acc_ref[rows, :] = jnp.zeros((block, d), F32)

    @pl.when((step >= 2) & (step <= tiles))
    def _():
        for copy in put_gu(step - 2):
            copy.wait()

    @pl.when(n == 0)
    def _():
        for copy in put_gu(tiles - 1):
            copy.wait()
        load_dy().wait()

    @pl.when((n >= tiles - 1) & (n < 2 * tiles - 1))
    def _():
        for copy in get_gu(n + 1 - tiles):
            copy.start()

    def gu(c, a, slot):
        rows = pl.ds(c * mc, mc)
        a = a[rows, :]
        g_ref[slot, rows, :] = dot(a, wg_ref[0])
        u_ref[slot, rows, :] = dot(a, wu_ref[0])

    def da(c, right):
        dact_ref[c % 2] = dot_t(right[pl.ds(c * mc, mc), :], wd_ref[0])

    def epi(c, slot):
        rows = pl.ds(c * mc, mc)
        dact = dact_ref[c % 2].astype(BF16).astype(F32)
        act, dgate, dup = gates(g_ref[slot, rows, :], u_ref[slot, rows, :], dact)
        act_ref[rows, :] = act
        dgu_ref[rows, :tn] = dgate
        dgu_ref[rows, tn:] = dup

    term = [jnp.where(place.core == c, lax.rem(n + 2 * OWN, OWN), OWN + lax.rem(n + 2 * OWN, 2)) for c in range(2)]

    def weights_down(right):
        lanes = d // (2 * side)
        down = t_dot(act_ref[...], right[...]).astype(BF16)
        for o in range(2):
            for c in range(2):
                for i in range(side):
                    for j in range(side):
                        k = (i * side + j) * piece
                        own[term[c], o, k:k + piece, tn:] = down[
                            (o * side + i) * piece:(o * side + i + 1) * piece, (c * side + j) * lanes:(c * side + j + 1) * lanes
                        ]

    def weights_in(left, c):
        half = d // 2
        at = left[:, c * half:(c + 1) * half]
        own[term[c], 0, :, :tn] = t_dot(at, dgu_ref[:, :tn]).astype(BF16)
        own[term[c], 1, :, :tn] = t_dot(at, dgu_ref[:, tn:]).astype(BF16)

    @pl.when(n < 0)
    def _():
        slot = lax.rem(step, 2)

        def silu(c):
            rows = pl.ds(c * mc, mc)
            g, u = g_ref[slot, rows, :], u_ref[slot, rows, :]
            act_ref[rows, :] = (g * jax.nn.sigmoid(g) * u).astype(BF16)

        def down(c):
            rows = pl.ds(c * mc, mc)
            acc_ref[rows, :] += dot(act_ref[rows, :], wd_ref[0])

        gu(0, a0_ref, slot)
        for c in range(chunks):
            if c + 1 < chunks:
                gu(c + 1, a0_ref, slot)
            silu(c)
            if c > 0:
                down(c - 1)
        down(chunks - 1)
        for copy in put_gu(step):
            copy.start()

    @pl.when(n == -1)
    def _():
        @pl.loop(0, blocks)
        def _(i):
            rows = ds(i, block)
            y = acc_ref[rows, :].astype(BF16).astype(F32)
            h = (h_ref[rows, :].astype(F32) + y).astype(BF16)
            h_ref[rows, :] = h
            a_ref[rows, :] = norm_rows(h)
            acc_ref[rows, :] = jnp.zeros((block, d), F32)

    @pl.when((n >= 0) & (n < tiles))
    def _():
        def back(c):
            rows = pl.ds(c * mc, mc)
            acc_ref[rows, :] += dot_t(dgu_ref[rows, :tn], wg_ref[0]) + dot_t(dgu_ref[rows, tn:], wu_ref[0])

        gu(0, a_ref, 0)
        da(0, dy_ref)
        for c in range(1, chunks):
            gu(c, a_ref, 0)
            da(c, dy_ref)
            epi(c - 1, 0)
        back(0)
        epi(chunks - 1, 0)
        for c in range(1, chunks):
            back(c)
        exchange.tick(2 * n)
        weights_down(dy_ref)
        weights_in(a_ref, 0)
        weights_in(a_ref, 1)

    @pl.when((n >= tiles) & (n < 2 * tiles))
    def _():
        slot = lax.rem(n - tiles + 1, 2)
        for copy in get_gu(n - tiles):
            copy.wait()
        da(0, h_ref)
        for c in range(1, chunks):
            da(c, h_ref)
            epi(c - 1, slot)
        epi(chunks - 1, slot)
        weights_down(h_ref)
        weights_in(a0_ref, 0)
        weights_in(a0_ref, 1)

    @pl.when(n >= 0)
    def _():
        exchange.tick(jnp.where(n < tiles, 2 * n + 1, n + tiles))

    @pl.when(n == tiles - 1)
    def _():
        @pl.loop(0, blocks)
        def _(i):
            rows = ds(i, block)
            da = acc_ref[rows, :].astype(BF16).astype(F32)
            h = h_ref[rows, :].astype(F32)
            ms = jnp.mean(h * h, -1, keepdims=True) + 1e-6
            r = lax.rsqrt(ms)
            along = jnp.mean(da * h, -1, keepdims=True)
            dn = (r * (da - h * (along / ms))).astype(BF16).astype(F32)
            h_ref[rows, :] = (dy_ref[rows, :].astype(F32) + dn).astype(BF16)

    @pl.when(n == 2 * tiles - 1 + FINISH)
    def _():
        squares = Total(place, sums, vs, vr)
        value = jnp.full(factor_ref.shape, jnp.sum(sq_ref[...]), F32)
        for k in range(2):
            value = squares.over(k, value)
        factor_ref[...] = jnp.minimum(1.0, 0.5 * lax.rsqrt(value / count + 1e-30))


def layers(x, dy, wg, wu, wd, tn, side, gathered, count):
    t, d = x.shape
    ff = wg.shape[2]
    tiles = ff // tn
    piece, wide = d // (2 * side * side), tn + d // (2 * side)
    chunk = side * piece
    rows = side * chunk
    mc = t // 4
    hbm = pl.BlockSpec(memory_space=pl.ANY)
    layer = lambda n: jnp.where(n < tiles, 0, 1)
    tile = lambda n: jnp.where(n < tiles, n, jnp.minimum(n - tiles, tiles - 1))
    rest = (2 * tiles - gathered, 2, piece, wide)
    return pl.pallas_call(
        functools.partial(layers_kernel, mc=mc, side=side, tiles=tiles, gathered=gathered, count=count),
        grid=(3 * tiles + FINISH,),
        in_specs=[
            hbm,
            hbm,
            pl.BlockSpec((1, d, tn), lambda n: (layer(n), 0, tile(n))),
            pl.BlockSpec((1, d, tn), lambda n: (layer(n), 0, tile(n))),
            pl.BlockSpec((1, tn, d), lambda n: (
                jnp.where((n >= tiles) & (n < 2 * tiles), 1, 0), jnp.where(n < 3 * tiles, lax.rem(n, tiles), tiles - 1), 0
            )),
        ],
        out_specs=[
            hbm,
            pl.BlockSpec(rest, lambda n: (0, 0, 0, 0), **ONE),
            pl.BlockSpec((8, 128), lambda n: (0, 0), **ONE),
            hbm,
            hbm,
        ],
        out_shape=[
            jax.ShapeDtypeStruct((gathered, 2, 2, side * side, piece, wide), BF16),
            jax.ShapeDtypeStruct(rest, BF16),
            jax.ShapeDtypeStruct((8, 128), F32),
            jax.ShapeDtypeStruct((tiles, t, tn), F32),
            jax.ShapeDtypeStruct((tiles, t, tn), F32),
        ],
        scratch_shapes=[
            *[pltpu.VMEM((t, d), BF16)] * 4, pltpu.VMEM((t, d), F32),
            pltpu.VMEM((2, t, tn), F32), pltpu.VMEM((2, t, tn), F32), pltpu.VMEM((2, mc, tn), F32),
            pltpu.VMEM((t, tn), BF16), pltpu.VMEM((t, 2 * tn), BF16),
            pltpu.VMEM((OWN + 2, 2, rows, wide), BF16),
            pltpu.VMEM((MATE, 2, rows, wide), BF16),
            pltpu.VMEM((2, 2, (chunk + piece) * 3 // 2, wide), BF16),
            pltpu.VMEM((DEPTH, 2, 2, (chunk + piece) * 3 // 2, wide), BF16),
            pltpu.VMEM((DEPTH, 2, chunk, wide), F32),
            pltpu.VMEM((2 * tiles, 2, piece, wide), BF16),
            pltpu.VMEM((piece, wide), F32),
            pltpu.VMEM((2, 2 * side, 8, 128), F32),
            DMA((8,)), DMA, DMA((2, 2)), DMA((2, 2 * side)), DMA((2, 2 * side)), DMA((DEPTH, 2)),
            DMA((2,)), DMA((MATE,)),
            *[sem for name in range(6) for sem in (DMA, DMA((DEPTH,)))],
        ],
        compiler_params=pltpu.CompilerParams(
            vmem_limit_bytes=VLIM, dimension_semantics=("arbitrary",), collective_id=0, has_side_effects=True
        ),
        cost_estimate=pl.CostEstimate(flops=30 * t * d * ff, bytes_accessed=24 * d * ff, transcendentals=3 * t * ff),
        name="layers",
    )(x, dy, wg, wu, wd)[:3]


def adam_kernel(factor_ref, grad_ref, *refs, side, own):
    weights, moments, squares, new_w, new_m, new_v = (refs[i:i + 3] for i in [*range(0, 9, 3), *range(len(refs) - 9, len(refs), 3)])
    piece, wide = grad_ref.shape[-2:]
    tn = new_w[0].shape[2]
    lanes = wide - tn
    f = factor_ref[0, 0]

    def grad(c, o, i, j):
        if own:
            return grad_ref.at[0, c, o, i * side + j]
        return grad_ref.at[((i * side + j) if o == 0 else (j * side + i)) * 2 + c, 0, o]

    def step(k, at, g):
        g = g.astype(F32) * f
        m = 0.9 * moments[k][at] + 0.1 * g
        v = 0.95 * squares[k][at] + 0.05 * (g * g)
        w = weights[k][at].astype(F32)
        new_w[k][at] = (w - 0.02 * (m * lax.rsqrt(v + 1e-8) + 0.1 * w)).astype(BF16)
        new_m[k][at] = m
        new_v[k][at] = v

    for c in range(2):
        @pl.loop(0, side)
        def _(i):
            for j in range(side):
                for o in range(2):
                    step(o, (0, ds((c * side + i) * side + j, piece), slice(None)), grad(c, o, i, j)[:, :tn])
            for o in range(2):
                for j in range(side):
                    at = (0, ds(o * side + i, piece), slice((c * side + j) * lanes, (c * side + j + 1) * lanes))
                    step(2, at, grad(c, o, i, j)[:, tn:])


def adam(factor, grad, ws, ms, vs, so_far, tn, side, first, count):
    _, d, ff = ws[0].shape
    tiles = ff // tn
    at = lambda t: (1 - (t + first) // tiles, (t + first) % tiles)
    up = pl.BlockSpec((1, d, tn), lambda t: (at(t)[0], 0, at(t)[1]))
    down = pl.BlockSpec((1, tn, d), lambda t: (*at(t), 0))
    blocks = [up, up, down]
    own = not so_far
    size = sum(w.size for w in ws) * count // (2 * tiles)
    if own:
        grad_block = pl.BlockSpec((1, *grad.shape[1:]), lambda t: (t, 0, 0, 0, 0, 0))
    else:
        grad_block = pl.BlockSpec((grad.shape[0], 1, *grad.shape[2:]), lambda t: (0, t, 0, 0, 0))
    out = pl.pallas_call(
        functools.partial(adam_kernel, side=side, own=own),
        grid=(count,),
        in_specs=[
            pl.BlockSpec(factor.shape, lambda t: (0, 0), **ONE),
            grad_block,
            *blocks * 3,
            *[pl.BlockSpec(memory_space=pl.ANY)] * len(so_far),
        ],
        out_specs=blocks * 3,
        out_shape=[jax.ShapeDtypeStruct(a.shape, a.dtype) for a in (*ws, *ms, *vs)],
        input_output_aliases={11 + i: i for i in range(len(so_far))},
        compiler_params=pltpu.CompilerParams(vmem_limit_bytes=VLIM, dimension_semantics=("arbitrary",)),
        cost_estimate=pl.CostEstimate(flops=20 * size, bytes_accessed=22 * size, transcendentals=size),
        name="adam_own" if own else "adam_rest",
    )(factor, grad, *ws, *ms, *vs, *so_far)
    return tuple(out)


def solution(mesh):
    side = math.isqrt(mesh.shape["dp"] // 2)

    def step(x, dy, *arrays):
        ws, ms, vs = (arrays[i:i + 3] for i in (0, 3, 6))
        x, dy = x[0], dy[0]
        tn = x.shape[1] // side
        tiles = ws[0].shape[0] * ws[0].shape[2] // tn
        gathered = tiles * 6 // 10
        full, rest, factor = layers(x, dy, *ws, tn, side, gathered, sum(w.size for w in ws))
        rest = lax.all_gather(rest, "dp")
        new = adam(factor, full, ws, ms, vs, (), tn, side, 0, gathered)
        return adam(factor, rest, ws, ms, vs, new, tn, side, gathered, tiles - gathered)

    return jax.shard_map(
        step,
        mesh=mesh,
        in_specs=(P(("rep", "dp"), None, None),) * 2 + (P(None, None, None),) * 9,
        out_specs=(P("rep", None, None),) * 9,
        check_vma=False,
    )
```

time: 706 us -> 394 us (0.56); the launches traced: 697 us -> 394 us
  Pallas kernels: 0 us -> 380 us
  matrix products: 298 us -> 0 us
  waiting for transfers between devices: 226 us -> 0.08 us
  other arithmetic: 143 us -> 0 us
  local copies, waits for them, and re-layouts: 13.2 us -> 0 us
    pallas_call x0 -> x3, Pallas kernels: none -> 380 us  [the longest x1 266 us: layers(): pl.pallas_call(functools.partial(layers_kernel, mc=mc, side=side, tiles=t...]
    dot_general x15 -> x0, matrix products: 298 us -> none  [the longest x5 105 us: layer(): up = jnp.dot(a, w['w_up'], preferred_element_type=jnp.float32)]
    psum x1 -> x0, waiting for transfers between devices: 226 us -> none  [step(): summed[number] = [lax.psum(by_w[name], 'dp') for name in NAMES]]
    convert_element_type x2 -> x0, other arithmetic: 113 us -> none  [adamw(): return ((w - 0.02 * step).astype(jnp.bfloat16), m, v)]
    reduce_sum x4 -> x0, other arithmetic: 27 us -> none  [the longest x3 24 us: step(): jnp.sum(g * g)]
    unnamed x30 -> x0, local copies, waits for them, and re-layouts: 13.2 us -> none
  transfers between devices with their start and end apart: 1 -> 1, of which waited for: 1 -> 0; matrix products, arithmetic and copies ran while one was open for 0% -> 0% of each run, Pallas kernels for 0% -> 17%
where the time goes in v2:
time: 394 us
  Pallas kernels  380 us (96%)
  between operations  14.1 us (4%)
    pallas_call x1, Pallas kernels, layers(): pl.pallas_call(functools.partial(layers_kernel, mc=mc, side=side, tiles=t...  266 us
    pallas_call x2, Pallas kernels, adam(): pl.pallas_call(functools.partial(adam_kernel, side=side, own=own), grid=(...  114 us
  transfers between devices with their start and end apart: 1, of which 0 were waited for; matrix products, arithmetic and copies ran while one was open for 0% of the time, Pallas kernels for 17%

profile of v2, /device:TPU:97, one launch (start us, length us, event | category | flops | bytes accessed | tf_op | source)
XLA Modules:
  0.0 394.3 jit_solution(8454589386379248879)
XLA Ops:
  7.2 0.1 all-gather.3.cloned.1.call-start
  7.3 266.1 %layers.1 = (bf16[12,2,2,16,32,384]{5,4,3,2,1,0:T(8,128)(2,1)}, bf16[8,2,32,384]{3,2,1,0:T(8,128)(2,1)}, f32[8,128]{1,0:T(8,128)}, f32[10,2048,256]{2,1,0:T(8,128)}, f32[10,2048,256]{2,1,0:T(8,128)}) custom-call(bf16[2048,1024]{1,0:T(8,128)(2,1)} %bitcast.4, bf16[2048,1024]{1,0:T(8,128)(2,1)} %bitcast.5, bf16[2,1024,2560]{2,1,0:T(8,128)(2,1)} %refs_0_.3, ...), custom_call_target="tpu_custom_call" | custom-call | flops 161061273600 | bytes 62914560 | tf_op jit(solution)/shard_map/layers/pallas_call | solution.py:571
  273.3 0.1 all-gather.3.cloned.1.call-update
  273.4 68.5 %adam_own.1 = (bf16[2,1024,2560]{2,1,0:T(8,128)(2,1)}, bf16[2,1024,2560]{2,1,0:T(8,128)(2,1)}, bf16[2,2560,1024]{2,1,0:T(8,128)(2,1)}, f32[2,1024,2560]{2,1,0:T(...) custom-call(f32[8,128]{1,0:T(8,128)} %get-tuple-element.21.factor_re, ...), custom_call_target="tpu_custom_call" | custom-call | flops 188743680 | bytes 207618048 | tf_op jit(solution)/shard_map/adam_own/pallas_call | solution.py:667
  341.9 0.0 all-gather.3.cloned.1.call-done
  341.9 45.5 %adam_rest.1 = (bf16[2,1024,2560]{2,1,0:T(8,128)(2,1)}, bf16[2,1024,2560]{2,1,0:T(8,128)(2,1)}, bf16[2,2560,1024]{2,1,0:T(8,128)(2,1)}, f32[2,1024,2560]{2,1,0:T...) custom-call(f32[8,128]{1,0:T(8,128)} %get-tuple-element.21.factor_re, ...), custom_call_target="tpu_custom_call", output_to_operand_aliasing={{0}: (11, {}), {1}: (12, {}), {2}: (13, {}), {3}: (14, {}),... | custom-call | flops 125829120 | bytes 138412032 | tf_op jit(solution)/shard_map/adam_rest/pallas_call | solution.py:667
Async XLA Ops:
  7.2 334.7 %all-gather.3.cloned.1.call-start = ((), (), s32[]{:S(2)}) async-start(), calls=%async_computation | async-start | bytes 12976128 | tf_op jit(solution)/shard_map/all_gather | solution.py:696
Sparse Core Ops, SparseCore 0:
  273.5 57.0 all-gather.2

commit v3 on v2

--- a/solution.py
+++ b/solution.py
@@ -355,12 +355,10 @@
     return act, dgate, dup
 
 
-def layers_kernel(x_hbm, dy_hbm, wg_ref, wu_ref, wd_ref, full_ref, rest_ref, factor_ref, gate_hbm, up_hbm,
-                  dy_ref, h_ref, a_ref, a0_ref, acc_ref, g_ref, u_ref, dact_ref, act_ref, dgu_ref,
+def layers_kernel(x_hbm, dy_hbm, wg_hbm, wu_hbm, wd_hbm, full_ref, rest_ref, factor_ref, gate_hbm, up_hbm,
+                  wg_ref, wu_ref, wd_ref, dy_ref, h_ref, a_ref, a0_ref, acc_ref, g_ref, u_ref, dact_ref, act_ref, dgu_ref,
                   own, mate, out, inn, total, shard_ref, sq_ref, sums,
-                  x_sem, dy_sem, gu_sem, vs, vr, keep_sem, *pairs, mc, side, tiles, gathered, count):
-    step = pl.program_id(0)
-    n = step - tiles
+                  w_sem, x_sem, dy_sem, gu_sem, vs, vr, keep_sem, *pairs, mc, side, tiles, gathered, count):
     tokens, d = h_ref.shape
     tn = wg_ref.shape[2]
     chunks, blocks = tokens // mc, x_sem.shape[0]
@@ -378,59 +376,52 @@
     def load_dy():
         return pltpu.make_async_copy(dy_hbm, dy_ref, dy_sem)
 
+    def load_in(layer, t):
+        slot = lax.rem(t, 2)
+        return [
+            pltpu.make_async_copy(wg_hbm.at[layer, :, ds(t, tn)], wg_ref.at[slot], w_sem.at[slot, 0]),
+            pltpu.make_async_copy(wu_hbm.at[layer, :, ds(t, tn)], wu_ref.at[slot], w_sem.at[slot, 1]),
+        ]
+
+    def load_down(layer, t):
+        slot = lax.rem(t, 2)
+        return [pltpu.make_async_copy(wd_hbm.at[layer, ds(t, tn)], wd_ref.at[slot], w_sem.at[slot, 2])]
+
     def put_gu(t):
         slot = lax.rem(t, 2)
-        return (
+        return [
             pltpu.make_async_copy(g_ref.at[slot], gate_hbm.at[t], gu_sem.at[slot, 0]),
             pltpu.make_async_copy(u_ref.at[slot], up_hbm.at[t], gu_sem.at[slot, 1]),
-        )
+        ]
 
     def get_gu(t):
         slot = lax.rem(t + 1, 2)
-        return (
+        return [
             pltpu.make_async_copy(gate_hbm.at[t], g_ref.at[slot], gu_sem.at[slot, 0]),
             pltpu.make_async_copy(up_hbm.at[t], u_ref.at[slot], gu_sem.at[slot, 1]),
-        )
-
-    @pl.when(step == 0)
-    def _():
-        for i in range(blocks):
-            load_x(i).start()
-        load_dy().start()
-        greet([*place.members[0][1:], *place.members[1][1:]])
-        sq_ref[...] = jnp.zeros_like(sq_ref)
-
-        @pl.loop(0, blocks)
-        def _(i):
-            rows = ds(i, block)
-            load_x(i).wait()
-            a0_ref[rows, :] = norm_rows(h_ref[rows, :])
-            acc_ref[rows, :] = jnp.zeros((block, d), F32)
-
-    @pl.when((step >= 2) & (step <= tiles))
-    def _():
-        for copy in put_gu(step - 2):
+        ]
+
+    def start(copies):
+        for copy in copies:
+            copy.start()
+
+    def wait(copies):
+        for copy in copies:
             copy.wait()
 
-    @pl.when(n == 0)
-    def _():
-        for copy in put_gu(tiles - 1):
-            copy.wait()
-        load_dy().wait()
-
-    @pl.when((n >= tiles - 1) & (n < 2 * tiles - 1))
-    def _():
-        for copy in get_gu(n + 1 - tiles):
-            copy.start()
-
-    def gu(c, a, slot):
+    def ahead(layer, t, what):
+        for load in what:
+            pl.when(t + 1 < tiles)(lambda load=load: start(load(layer, t + 1)))
+            wait(load(layer, t))
+
+    def gu(c, t, a, slot):
         rows = pl.ds(c * mc, mc)
         a = a[rows, :]
-        g_ref[slot, rows, :] = dot(a, wg_ref[0])
-        u_ref[slot, rows, :] = dot(a, wu_ref[0])
-
-    def da(c, right):
-        dact_ref[c % 2] = dot_t(right[pl.ds(c * mc, mc), :], wd_ref[0])
+        g_ref[slot, rows, :] = dot(a, wg_ref[lax.rem(t, 2)])
+        u_ref[slot, rows, :] = dot(a, wu_ref[lax.rem(t, 2)])
+
+    def da(c, t, right):
+        dact_ref[c % 2] = dot_t(right[pl.ds(c * mc, mc), :], wd_ref[lax.rem(t, 2)])
 
     def epi(c, slot):
         rows = pl.ds(c * mc, mc)
@@ -440,10 +431,9 @@
         dgu_ref[rows, :tn] = dgate
         dgu_ref[rows, tn:] = dup
 
-    term = [jnp.where(place.core == c, lax.rem(n + 2 * OWN, OWN), OWN + lax.rem(n + 2 * OWN, 2)) for c in range(2)]
-
-    def weights_down(right):
-        lanes = d // (2 * side)
+    def terms(n, left, right):
+        term = [jnp.where(place.core == c, lax.rem(n, OWN), OWN + lax.rem(n, 2)) for c in range(2)]
+        lanes, half = d // (2 * side), d // 2
         down = t_dot(act_ref[...], right[...]).astype(BF16)
         for o in range(2):
             for c in range(2):
@@ -453,16 +443,30 @@
                         own[term[c], o, k:k + piece, tn:] = down[
                             (o * side + i) * piece:(o * side + i + 1) * piece, (c * side + j) * lanes:(c * side + j + 1) * lanes
                         ]
-
-    def weights_in(left, c):
-        half = d // 2
-        at = left[:, c * half:(c + 1) * half]
-        own[term[c], 0, :, :tn] = t_dot(at, dgu_ref[:, :tn]).astype(BF16)
-        own[term[c], 1, :, :tn] = t_dot(at, dgu_ref[:, tn:]).astype(BF16)
-
-    @pl.when(n < 0)
-    def _():
-        slot = lax.rem(step, 2)
+        for c in range(2):
+            at = left[:, c * half:(c + 1) * half]
+            own[term[c], 0, :, :tn] = t_dot(at, dgu_ref[:, :tn]).astype(BF16)
+            own[term[c], 1, :, :tn] = t_dot(at, dgu_ref[:, tn:]).astype(BF16)
+
+    for i in range(blocks):
+        load_x(i).start()
+    start(load_in(0, 0) + load_down(0, 0))
+    load_dy().start()
+    greet([*place.members[0][1:], *place.members[1][1:]])
+    sq_ref[...] = jnp.zeros_like(sq_ref)
+
+    @pl.loop(0, blocks)
+    def _(i):
+        rows = ds(i, block)
+        load_x(i).wait()
+        a0_ref[rows, :] = norm_rows(h_ref[rows, :])
+        acc_ref[rows, :] = jnp.zeros((block, d), F32)
+
+    @pl.loop(0, tiles)
+    def _(t):
+        slot = lax.rem(t, 2)
+        pl.when(t >= 2)(lambda: wait(put_gu(t - 2)))
+        ahead(0, t, (load_in, load_down))
 
         def silu(c):
             rows = pl.ds(c * mc, mc)
@@ -471,89 +475,91 @@
 
         def down(c):
             rows = pl.ds(c * mc, mc)
-            acc_ref[rows, :] += dot(act_ref[rows, :], wd_ref[0])
-
-        gu(0, a0_ref, slot)
+            acc_ref[rows, :] += dot(act_ref[rows, :], wd_ref[slot])
+
+        gu(0, t, a0_ref, slot)
         for c in range(chunks):
             if c + 1 < chunks:
-                gu(c + 1, a0_ref, slot)
+                gu(c + 1, t, a0_ref, slot)
             silu(c)
             if c > 0:
                 down(c - 1)
         down(chunks - 1)
-        for copy in put_gu(step):
-            copy.start()
-
-    @pl.when(n == -1)
-    def _():
-        @pl.loop(0, blocks)
-        def _(i):
-            rows = ds(i, block)
-            y = acc_ref[rows, :].astype(BF16).astype(F32)
-            h = (h_ref[rows, :].astype(F32) + y).astype(BF16)
-            h_ref[rows, :] = h
-            a_ref[rows, :] = norm_rows(h)
-            acc_ref[rows, :] = jnp.zeros((block, d), F32)
-
-    @pl.when((n >= 0) & (n < tiles))
-    def _():
+        start(put_gu(t))
+
+    start(load_in(1, 0) + load_down(1, 0))
+
+    @pl.loop(0, blocks)
+    def _(i):
+        rows = ds(i, block)
+        y = acc_ref[rows, :].astype(BF16).astype(F32)
+        h = (h_ref[rows, :].astype(F32) + y).astype(BF16)
+        h_ref[rows, :] = h
+        a_ref[rows, :] = norm_rows(h)
+        acc_ref[rows, :] = jnp.zeros((block, d), F32)
+
+    wait(put_gu(tiles - 2) + put_gu(tiles - 1) + [load_dy()])
+    start(get_gu(0))
+
+    @pl.loop(0, tiles)
+    def _(n):
+        ahead(1, n, (load_in, load_down))
+
         def back(c):
             rows = pl.ds(c * mc, mc)
-            acc_ref[rows, :] += dot_t(dgu_ref[rows, :tn], wg_ref[0]) + dot_t(dgu_ref[rows, tn:], wu_ref[0])
-
-        gu(0, a_ref, 0)
-        da(0, dy_ref)
+            slot = lax.rem(n, 2)
+            acc_ref[rows, :] += dot_t(dgu_ref[rows, :tn], wg_ref[slot]) + dot_t(dgu_ref[rows, tn:], wu_ref[slot])
+
+        gu(0, n, a_ref, 0)
+        da(0, n, dy_ref)
         for c in range(1, chunks):
-            gu(c, a_ref, 0)
-            da(c, dy_ref)
+            gu(c, n, a_ref, 0)
+            da(c, n, dy_ref)
             epi(c - 1, 0)
         back(0)
         epi(chunks - 1, 0)
         for c in range(1, chunks):
             back(c)
         exchange.tick(2 * n)
-        weights_down(dy_ref)
-        weights_in(a_ref, 0)
-        weights_in(a_ref, 1)
-
-    @pl.when((n >= tiles) & (n < 2 * tiles))
-    def _():
-        slot = lax.rem(n - tiles + 1, 2)
-        for copy in get_gu(n - tiles):
-            copy.wait()
-        da(0, h_ref)
+        terms(n, a_ref, dy_ref)
+        exchange.tick(2 * n + 1)
+
+    start(load_down(0, 0))
+
+    @pl.loop(0, blocks)
+    def _(i):
+        rows = ds(i, block)
+        da = acc_ref[rows, :].astype(BF16).astype(F32)
+        h = h_ref[rows, :].astype(F32)
+        ms = jnp.mean(h * h, -1, keepdims=True) + 1e-6
+        r = lax.rsqrt(ms)
+        along = jnp.mean(da * h, -1, keepdims=True)
+        dn = (r * (da - h * (along / ms))).astype(BF16).astype(F32)
+        h_ref[rows, :] = (dy_ref[rows, :].astype(F32) + dn).astype(BF16)
+
+    @pl.loop(0, tiles)
+    def _(t):
+        slot = lax.rem(t + 1, 2)
+        ahead(0, t, (load_down,))
+        pl.when(t + 1 < tiles)(lambda: start(get_gu(t + 1)))
+        wait(get_gu(t))
+        da(0, t, h_ref)
         for c in range(1, chunks):
-            da(c, h_ref)
+            da(c, t, h_ref)
             epi(c - 1, slot)
         epi(chunks - 1, slot)
-        weights_down(h_ref)
-        weights_in(a0_ref, 0)
-        weights_in(a0_ref, 1)
-
-    @pl.when(n >= 0)
-    def _():
-        exchange.tick(jnp.where(n < tiles, 2 * n + 1, n + tiles))
-
-    @pl.when(n == tiles - 1)
-    def _():
-        @pl.loop(0, blocks)
-        def _(i):
-            rows = ds(i, block)
-            da = acc_ref[rows, :].astype(BF16).astype(F32)
-            h = h_ref[rows, :].astype(F32)
-            ms = jnp.mean(h * h, -1, keepdims=True) + 1e-6
-            r = lax.rsqrt(ms)
-            along = jnp.mean(da * h, -1, keepdims=True)
-            dn = (r * (da - h * (along / ms))).astype(BF16).astype(F32)
-            h_ref[rows, :] = (dy_ref[rows, :].astype(F32) + dn).astype(BF16)
-
-    @pl.when(n == 2 * tiles - 1 + FINISH)
-    def _():
-        squares = Total(place, sums, vs, vr)
-        value = jnp.full(factor_ref.shape, jnp.sum(sq_ref[...]), F32)
-        for k in range(2):
-            value = squares.over(k, value)
-        factor_ref[...] = jnp.minimum(1.0, 0.5 * lax.rsqrt(value / count + 1e-30))
+        terms(tiles + t, a0_ref, h_ref)
+        exchange.tick(2 * tiles + t)
+
+    @pl.loop(0, FINISH)
+    def _(i):
+        exchange.tick(3 * tiles + i)
+
+    squares = Total(place, sums, vs, vr)
+    value = jnp.full(factor_ref.shape, jnp.sum(sq_ref[...]), F32)
+    for k in range(2):
+        value = squares.over(k, value)
+    factor_ref[...] = jnp.minimum(1.0, 0.5 * lax.rsqrt(value / count + 1e-30))
 
 
 def layers(x, dy, wg, wu, wd, tn, side, gathered, count):
@@ -565,28 +571,11 @@
     rows = side * chunk
     mc = t // 4
     hbm = pl.BlockSpec(memory_space=pl.ANY)
-    layer = lambda n: jnp.where(n < tiles, 0, 1)
-    tile = lambda n: jnp.where(n < tiles, n, jnp.minimum(n - tiles, tiles - 1))
     rest = (2 * tiles - gathered, 2, piece, wide)
     return pl.pallas_call(
         functools.partial(layers_kernel, mc=mc, side=side, tiles=tiles, gathered=gathered, count=count),
-        grid=(3 * tiles + FINISH,),
-        in_specs=[
-            hbm,
-            hbm,
-            pl.BlockSpec((1, d, tn), lambda n: (layer(n), 0, tile(n))),
-            pl.BlockSpec((1, d, tn), lambda n: (layer(n), 0, tile(n))),
-            pl.BlockSpec((1, tn, d), lambda n: (
-                jnp.where((n >= tiles) & (n < 2 * tiles), 1, 0), jnp.where(n < 3 * tiles, lax.rem(n, tiles), tiles - 1), 0
-            )),
-        ],
-        out_specs=[
-            hbm,
-            pl.BlockSpec(rest, lambda n: (0, 0, 0, 0), **ONE),
-            pl.BlockSpec((8, 128), lambda n: (0, 0), **ONE),
-            hbm,
-            hbm,
-        ],
+        in_specs=[hbm] * 5,
+        out_specs=[hbm, pl.BlockSpec(memory_space=pltpu.VMEM), pl.BlockSpec(memory_space=pltpu.VMEM), hbm, hbm],
         out_shape=[
             jax.ShapeDtypeStruct((gathered, 2, 2, side * side, piece, wide), BF16),
             jax.ShapeDtypeStruct(rest, BF16),
@@ -595,6 +584,7 @@
             jax.ShapeDtypeStruct((tiles, t, tn), F32),
         ],
         scratch_shapes=[
+            pltpu.VMEM((2, d, tn), BF16), pltpu.VMEM((2, d, tn), BF16), pltpu.VMEM((2, tn, d), BF16),
             *[pltpu.VMEM((t, d), BF16)] * 4, pltpu.VMEM((t, d), F32),
             pltpu.VMEM((2, t, tn), F32), pltpu.VMEM((2, t, tn), F32), pltpu.VMEM((2, mc, tn), F32),
             pltpu.VMEM((t, tn), BF16), pltpu.VMEM((t, 2 * tn), BF16),
@@ -606,12 +596,12 @@
             pltpu.VMEM((2 * tiles, 2, piece, wide), BF16),
             pltpu.VMEM((piece, wide), F32),
             pltpu.VMEM((2, 2 * side, 8, 128), F32),
-            DMA((8,)), DMA, DMA((2, 2)), DMA((2, 2 * side)), DMA((2, 2 * side)), DMA((DEPTH, 2)),
+            DMA((2, 3)), DMA((8,)), DMA, DMA((2, 2)), DMA((2, 2 * side)), DMA((2, 2 * side)), DMA((DEPTH, 2)),
             DMA((2,)), DMA((MATE,)),
             *[sem for name in range(6) for sem in (DMA, DMA((DEPTH,)))],
         ],
         compiler_params=pltpu.CompilerParams(
-            vmem_limit_bytes=VLIM, dimension_semantics=("arbitrary",), collective_id=0, has_side_effects=True
+            vmem_limit_bytes=VLIM, collective_id=0, has_side_effects=True
         ),
         cost_estimate=pl.CostEstimate(flops=30 * t * d * ff, bytes_accessed=24 * d * ff, transcendentals=3 * t * ff),
         name="layers",

time: 394 us -> 392 us (level)
  no operation moved by 1% of the time
where the time goes in v3:
time: 392 us
  Pallas kernels  378 us (96%)
  between operations  14.1 us (4%)
    pallas_call x1, Pallas kernels, layers(): pl.pallas_call(functools.partial(layers_kernel, mc=mc, side=side, tiles=t...  264 us
    pallas_call x2, Pallas kernels, adam(): pl.pallas_call(functools.partial(adam_kernel, side=side, own=own), grid=(...  114 us
  transfers between devices with their start and end apart: 1, of which 0 were waited for; matrix products, arithmetic and copies ran while one was open for 0% of the time, Pallas kernels for 17%

profile of v3, /device:TPU:97, one launch (start us, length us, event | category | flops | bytes accessed | tf_op | source)
XLA Modules:
  0.0 392.2 jit_solution(10074681228907982355)
XLA Ops:
  7.2 0.1 all-gather.3.cloned.1.call-start
  7.3 263.9 %layers.1 = (bf16[12,2,2,16,32,384]{5,4,3,2,1,0:T(8,128)(2,1)}, bf16[8,2,32,384]{3,2,1,0:T(8,128)(2,1)}, f32[8,128]{1,0:T(8,128)}, f32[10,2048,256]{2,1,0:T(8,128)}, f32[10,2048,256]{2,1,0:T(8,128)}) custom-call(bf16[2048,1024]{1,0:T(8,128)(2,1)} %bitcast.4, bf16[2048,1024]{1,0:T(8,128)(2,1)} %bitcast.5, bf16[2,1024,2560]{2,1,0:T(8,128)(2,1)} %refs_0_.3, ...), custom_call_target="tpu_custom_call" | custom-call | flops 161061273600 | bytes 62914560 | tf_op jit(solution)/shard_map/layers/pallas_call | solution.py:575
  271.2 0.1 all-gather.3.cloned.1.call-update
  271.3 68.5 %adam_own.1 = (bf16[2,1024,2560]{2,1,0:T(8,128)(2,1)}, bf16[2,1024,2560]{2,1,0:T(8,128)(2,1)}, bf16[2,2560,1024]{2,1,0:T(8,128)(2,1)}, f32[2,1024,2560]{2,1,0:T(...) custom-call(f32[8,128]{1,0:T(8,128)} %get-tuple-element.21.factor_re, ...), custom_call_target="tpu_custom_call" | custom-call | flops 188743680 | bytes 207618048 | tf_op jit(solution)/shard_map/adam_own/pallas_call | solution.py:657
  339.8 0.0 all-gather.3.cloned.1.call-done
  339.8 45.5 %adam_rest.1 = (bf16[2,1024,2560]{2,1,0:T(8,128)(2,1)}, bf16[2,1024,2560]{2,1,0:T(8,128)(2,1)}, bf16[2,2560,1024]{2,1,0:T(8,128)(2,1)}, f32[2,1024,2560]{2,1,0:T...) custom-call(f32[8,128]{1,0:T(8,128)} %get-tuple-element.21.factor_re, ...), custom_call_target="tpu_custom_call", output_to_operand_aliasing={{0}: (11, {}), {1}: (12, {}), {2}: (13, {}), {3}: (14, {}),... | custom-call | flops 125829120 | bytes 138412032 | tf_op jit(solution)/shard_map/adam_rest/pallas_call | solution.py:657
Async XLA Ops:
  7.2 332.6 %all-gather.3.cloned.1.call-start = ((), (), s32[]{:S(2)}) async-start(), calls=%async_computation | async-start | bytes 12976128 | tf_op jit(solution)/shard_map/all_gather | solution.py:686
Sparse Core Ops, SparseCore 0:
  271.4 57.0 all-gather.2

commit v4 on v3

--- a/solution.py
+++ b/solution.py
@@ -71,7 +71,7 @@
 
 
 OWN = 4
-MATE = 4
+MATE = 6
 DEPTH = 2
 GROUP = 2
 FINISH = 5
@@ -81,48 +81,53 @@
     def __init__(self, tiles, gathered, place, buffers, semaphores, shard_ref, full_ref, rest_ref, sq_ref):
         self.tiles, self.gathered, self.place = tiles, gathered, place
         self.early = tiles // 2
-        self.own, self.mate, self.out, self.inn, self.total = buffers
+        self.own, self.mate, self.out, self.inn, self.out2, self.inn2, self.total = buffers
         self.sems = semaphores
         self.shard, self.full, self.rest, self.sq = shard_ref, full_ref, rest_ref, sq_ref
         self.rows = self.mate.shape[2] // place.side
         self.sub = self.rows // place.side
-        half, small = self.rows // 2, self.sub // 2
-        self.a, self.a2, self.b2, self.b = 0, half, half + small, half + small + self.sub
+        self.b, self.b2 = self.rows // 2, self.sub // 2
 
     def tile(self, tick):
         two = tick < 2 * self.early
         there = (tick >= 0) & (tick < self.tiles + self.early) & ((lax.rem(tick + 4 * self.tiles, 2) == 1) | jnp.logical_not(two))
         return jnp.where(two, lax.div(tick, 2), tick - self.early), there
 
-    def neighbours(self):
-        return [(axis, k, self.place.first[axis][1 + k]) for axis in range(2) for k in range(2)]
-
-    def ring(self, tick, first, stop):
+    def ring(self, tick, o, one, two):
+        slot = lax.rem(tick, DEPTH)
+        copies = []
+        for rows, axis, out, inn, name in ((one, self.place.first, self.out, self.inn, 0), (two, self.place.second, self.out2, self.inn2, 1)):
+            if rows:
+                send, recv = self.sems["ring"]
+                at = pl.ds(rows[0], rows[1] - rows[0])
+                copies += [
+                    remote(out.at[o, k, at], inn.at[slot, o, k, at], send.at[o, name], recv.at[slot, o, name], axis[o][1 + k])
+                    for k in range(2)
+                ]
+        return copies
+
+    def ring_wait(self, tick, o, one, two):
         slot = lax.rem(tick, DEPTH)
         send, recv = self.sems["ring"]
-        rows = pl.ds(first, stop - first)
-        return [
-            remote(self.out.at[i, k, rows], self.inn.at[slot, i, k, rows], send, recv.at[slot], peer) for i, k, peer in self.neighbours()
-        ]
-
-    def ring_all(self, tick, first, stop, which):
-        slot = lax.rem(tick, DEPTH)
-        ref = self.inn.at[slot, :, :, pl.ds(first, stop - first)]
-        send, recv = self.sems["ring"]
-        return pltpu.make_async_copy(ref, ref, send if which == 0 else recv.at[slot])
+        for rows, inn, name in ((one, self.inn, 0), (two, self.inn2, 1)):
+            if rows:
+                ref = inn.at[slot, o, :, pl.ds(rows[0], rows[1] - rows[0])]
+                pltpu.make_async_copy(ref, ref, recv.at[slot, o, name]).wait()
+                pltpu.make_async_copy(ref, ref, send.at[o, name]).wait()
 
     def in_parts(self, tick, what):
-        end, middle, last = self.b + self.rows, 2 * self.early, self.tiles + self.early
+        middle, last = 2 * self.early, self.tiles + self.early
+        end, end2 = self.b + self.rows, self.b2 + self.sub
         odd = lax.rem(tick + 2, 2) == 1
-        for when, first, stop in (
-            ((tick >= 0) & (tick < middle) & jnp.logical_not(odd), self.a, self.b2),
-            ((tick >= 0) & (tick < middle) & odd, self.b2, end),
-            ((tick >= middle) & (tick <= last), self.a, end),
-            (tick == last + 1, self.a2, end),
-            (tick == last + 2, self.a2, self.b),
-            (tick == last + 3, self.b2, self.b),
+        for when, one, two in (
+            ((tick >= 0) & (tick < middle) & jnp.logical_not(odd), (0, self.b), (0, self.b2)),
+            ((tick >= 0) & (tick < middle) & odd, (self.b, end), (self.b2, end2)),
+            ((tick >= middle) & (tick <= last), (0, end), (0, end2)),
+            (tick == last + 1, (self.b, end), (0, end2)),
+            (tick == last + 2, None, (0, end2)),
+            (tick == last + 3, None, (self.b2, end2)),
         ):
-            pl.when(when)(functools.partial(what, first, stop))
+            pl.when(when)(functools.partial(what, one, two))
 
     def d2d(self, t):
         send, recv = self.sems["d2d"]
@@ -133,66 +138,58 @@
         at = pl.ds(pl.multiple_of(first, count), count)
         return self.own[lax.rem(t, OWN), o, at, :].astype(F32) + self.mate[lax.rem(t, MATE), o, at, :].astype(F32)
 
-    def sum_a(self, t, slot):
-        half = self.rows // 2
-        for o in range(2):
-            chunk = self.place.on(self.place.first[o][0], 2)
-            for i in range(0, self.rows, self.sub):
-                at = self.a + i % half
-                self.out[o, i // half, at:at + self.sub, :] = self.chip(t, o, chunk * self.rows + i, self.sub).astype(BF16)
-
-    def sum_b(self, t, slot, k):
-        half, side = self.rows // 2, self.place.side
-        for o in range(2):
-            chunk = self.place.on(self.place.first[o][0], (1, side - 1)[k])
+    def sum_a(self, t, o):
+        chunk = self.place.on(self.place.first[o][0], 2)
+        for i in range(0, self.rows, self.sub):
+            at = i % self.b
+            self.out[o, i // self.b, at:at + self.sub, :] = self.chip(t, o, chunk * self.rows + i, self.sub).astype(BF16)
+
+    def sum_b(self, t, slot, o):
+        for k in range(2):
+            chunk = self.place.on(self.place.first[o][0], (1, self.place.side - 1)[k])
             for i in range(0, self.rows, self.sub):
                 x = self.chip(t, o, chunk * self.rows + i, self.sub)
-                if i // half == k:
-                    at = self.a + i % half
+                if i // self.b == k:
+                    at = i % self.b
                     x = x + self.inn[slot, o, k, at:at + self.sub, :].astype(F32)
-                at = self.b + i
-                self.out[o, k, at:at + self.sub, :] = x.astype(BF16)
+                self.out[o, k, self.b + i:self.b + i + self.sub, :] = x.astype(BF16)
 
     def sum_a2(self, t, slot, o):
-        keep, half = lax.rem(t, DEPTH), self.sub // 2
+        keep, half = lax.rem(t, DEPTH), self.b2
         chunk = self.place.first[o][0]
         for i in range(0, self.rows, self.sub):
             x = self.chip(t, o, chunk * self.rows + i, self.sub)
-            at = self.b + i
             for k in range(2):
-                x = x + self.inn[slot, o, k, at:at + self.sub, :].astype(F32)
+                x = x + self.inn[slot, o, k, self.b + i:self.b + i + self.sub, :].astype(F32)
             self.total[keep, o, i:i + self.sub, :] = x
         far = self.place.on(self.place.second[o][0], 2)
         for k in range(2):
             x = self.total[keep, o, pl.ds(pl.multiple_of(far * self.sub + k * half, half), half), :]
-            self.out[1 - o, k, self.a2:self.a2 + half, :] = x.astype(BF16)
-
-    def sum_b2(self, t, slot):
-        keep, half, side = lax.rem(t, DEPTH), self.sub // 2, self.place.side
-        for o in range(2):
-            for k in range(2):
-                chunk = self.place.on(self.place.second[o][0], (1, side - 1)[k])
-                for i in range(2):
-                    x = self.total[keep, o, pl.ds(pl.multiple_of(chunk * self.sub + i * half, half), half), :]
-                    if i == k:
-                        x = x + self.inn[slot, 1 - o, k, self.a2:self.a2 + half, :].astype(F32)
-                    at = self.b2 + i * half
-                    self.out[1 - o, k, at:at + half, :] = x.astype(BF16)
-
-    def finish(self, t, slot):
-        keep = lax.rem(t, DEPTH)
-        for o in range(2):
-            x = self.total[keep, o, ds(self.place.second[o][0], self.sub), :]
-            for k in range(2):
-                x = x + self.inn[slot, 1 - o, k, self.b2:self.b2 + self.sub, :].astype(F32)
-            g = x.astype(BF16)
-            self.shard[t, o] = g
-            g = g.astype(F32)
-            self.sq[...] += g * g
+            self.out2[o, k, :half, :] = x.astype(BF16)
+
+    def sum_b2(self, t, slot, o):
+        keep, half = lax.rem(t, DEPTH), self.b2
+        for k in range(2):
+            chunk = self.place.on(self.place.second[o][0], (1, self.place.side - 1)[k])
+            for i in range(2):
+                x = self.total[keep, o, pl.ds(pl.multiple_of(chunk * self.sub + i * half, half), half), :]
+                if i == k:
+                    x = x + self.inn2[slot, o, k, :half, :].astype(F32)
+                self.out2[o, k, half + i * half:2 * half + i * half, :] = x.astype(BF16)
+
+    def finish(self, t, slot, o):
+        x = self.total[lax.rem(t, DEPTH), o, ds(self.place.second[o][0], self.sub), :]
+        for k in range(2):
+            x = x + self.inn2[slot, o, k, self.b2:, :].astype(F32)
+        g = x.astype(BF16)
+        self.shard[t, o] = g
 
         @pl.when(t >= self.gathered)
         def _():
-            self.rest[t - self.gathered] = self.shard[t]
+            self.rest[t - self.gathered, o] = g
+
+        g = g.astype(F32)
+        self.sq[...] += g * g
 
     def tiles_of(self, q):
         return pl.ds(q * GROUP, GROUP)
@@ -271,60 +268,46 @@
                 for copy in self.keep(q):
                     copy.start()
 
-    def tick(self, tick):
-        def ring_wait(first, stop):
-            self.ring_all(tick - 1, first, stop, 1).wait()
-            self.ring_all(tick - 1, first, stop, 0).wait()
-
-        def ring_start(first, stop):
-            for copy in self.ring(tick, first, stop):
+    def part(self, tick, o):
+        slot = lax.rem(tick + 1, DEPTH)
+        self.in_parts(tick - 1, functools.partial(self.ring_wait, tick - 1, o))
+
+        def at(back, what):
+            t, there = self.tile(tick - back)
+            pl.when(there)(lambda: what(t))
+
+        def first(t):
+            if o == 0:
+                self.d2d(t).wait_recv()
+                self.d2d(t).wait_send()
+            self.sum_a(t, o)
+
+        at(FINISH, lambda t: self.finish(t, slot, o))
+        at(2, lambda t: self.sum_b(t, slot, o))
+        at(1, first)
+        at(3, lambda t: self.sum_a2(t, slot, o))
+        at(4, lambda t: self.sum_b2(t, slot, o))
+
+        def ring_start(one, two):
+            for copy in self.ring(tick, o, one, two):
                 copy.start()
 
-        slot = lax.rem(tick + 1, DEPTH)
-        self.in_parts(tick - 1, ring_wait)
-
-        t5, there = self.tile(tick - FINISH)
-        pl.when(there)(lambda: self.finish(t5, slot))
-
-        t, there = self.tile(tick - 2)
-
-        @pl.when(there)
-        def _():
-            self.sum_b(t, slot, 0)
-            self.sum_b(t, slot, 1)
-
-        t1, there = self.tile(tick - 1)
-
-        @pl.when(there)
-        def _():
-            self.d2d(t1).wait_recv()
-            self.d2d(t1).wait_send()
-            self.sum_a(t1, slot)
-
-        t3, there = self.tile(tick - 3)
-
-        @pl.when(there)
-        def _():
-            self.sum_a2(t3, slot, 0)
-            self.sum_a2(t3, slot, 1)
-
-        t4, there = self.tile(tick - 4)
-
-        @pl.when(there)
-        def _():
-            self.sum_b2(t4, slot)
-
-        t0, there = self.tile(tick)
-
-        @pl.when(there)
-        def _():
-            self.d2d(t0).start()
-
         self.in_parts(tick, ring_start)
 
+    def cross(self, tick):
+        t, there = self.tile(tick)
+        pl.when(there)(lambda: self.d2d(t).start())
+
+    def others(self, tick):
         stages = ("d", "e", "f", "g", "h", "")
         for i in reversed(range(6)):
             self.gather_step(tick, i, stages[i - 1] if i else "", stages[i])
+
+    def tick(self, tick):
+        self.cross(tick)
+        self.part(tick, 0)
+        self.part(tick, 1)
+        self.others(tick)
 
 
 class Total:
@@ -357,7 +340,7 @@
 
 def layers_kernel(x_hbm, dy_hbm, wg_hbm, wu_hbm, wd_hbm, full_ref, rest_ref, factor_ref, gate_hbm, up_hbm,
                   wg_ref, wu_ref, wd_ref, dy_ref, h_ref, a_ref, a0_ref, acc_ref, g_ref, u_ref, dact_ref, act_ref, dgu_ref,
-                  own, mate, out, inn, total, shard_ref, sq_ref, sums,
+                  own, mate, out, inn, out2, inn2, total, shard_ref, sq_ref, sums,
                   w_sem, x_sem, dy_sem, gu_sem, vs, vr, keep_sem, *pairs, mc, side, tiles, gathered, count):
     tokens, d = h_ref.shape
     tn = wg_ref.shape[2]
@@ -367,7 +350,7 @@
     piece = d // (2 * side * side)
     sems = {name: pairs[2 * i:2 * i + 2] for i, name in enumerate(("d2d", "ring", "d", "e", "f", "g", "h"))}
     sems["keep"] = keep_sem
-    exchange = Exchange(2 * tiles, gathered, place, (own, mate, out, inn, total), sems, shard_ref, full_ref, rest_ref, sq_ref)
+    exchange = Exchange(2 * tiles, gathered, place, (own, mate, out, inn, out2, inn2, total), sems, shard_ref, full_ref, rest_ref, sq_ref)
 
     def load_x(i):
         rows = ds(i, block)
@@ -548,8 +531,11 @@
             da(c, t, h_ref)
             epi(c - 1, slot)
         epi(chunks - 1, slot)
+        exchange.part(2 * tiles + t, 0)
         terms(tiles + t, a0_ref, h_ref)
-        exchange.tick(2 * tiles + t)
+        exchange.cross(2 * tiles + t)
+        exchange.part(2 * tiles + t, 1)
+        exchange.others(2 * tiles + t)
 
     @pl.loop(0, FINISH)
     def _(i):
@@ -590,15 +576,17 @@
             pltpu.VMEM((t, tn), BF16), pltpu.VMEM((t, 2 * tn), BF16),
             pltpu.VMEM((OWN + 2, 2, rows, wide), BF16),
             pltpu.VMEM((MATE, 2, rows, wide), BF16),
-            pltpu.VMEM((2, 2, (chunk + piece) * 3 // 2, wide), BF16),
-            pltpu.VMEM((DEPTH, 2, 2, (chunk + piece) * 3 // 2, wide), BF16),
+            pltpu.VMEM((2, 2, chunk * 3 // 2, wide), BF16),
+            pltpu.VMEM((DEPTH, 2, 2, chunk * 3 // 2, wide), BF16),
+            pltpu.VMEM((2, 2, piece * 3 // 2, wide), BF16),
+            pltpu.VMEM((DEPTH, 2, 2, piece * 3 // 2, wide), BF16),
             pltpu.VMEM((DEPTH, 2, chunk, wide), F32),
             pltpu.VMEM((2 * tiles, 2, piece, wide), BF16),
             pltpu.VMEM((piece, wide), F32),
             pltpu.VMEM((2, 2 * side, 8, 128), F32),
             DMA((2, 3)), DMA((8,)), DMA, DMA((2, 2)), DMA((2, 2 * side)), DMA((2, 2 * side)), DMA((DEPTH, 2)),
-            DMA((2,)), DMA((MATE,)),
-            *[sem for name in range(6) for sem in (DMA, DMA((DEPTH,)))],
+            DMA((2,)), DMA((MATE,)), DMA((2, 2)), DMA((DEPTH, 2, 2)),
+            *[sem for name in range(5) for sem in (DMA, DMA((DEPTH,)))],
         ],
         compiler_params=pltpu.CompilerParams(
             vmem_limit_bytes=VLIM, collective_id=0, has_side_effects=True

time: 392 us -> 397 us (1.013)
  Pallas kernels: 378 us -> 383 us
    pallas_call x1, Pallas kernels: 264 us -> 269 us  [layers(): pl.pallas_call(functools.partial(layers_kernel, mc=mc, side=side, tiles=t...]
where the time goes in v4:
time: 397 us
  Pallas kernels  383 us (96%)
  between operations  14.1 us (4%)
    pallas_call x1, Pallas kernels, layers(): pl.pallas_call(functools.partial(layers_kernel, mc=mc, side=side, tiles=t...  269 us
    pallas_call x2, Pallas kernels, adam(): pl.pallas_call(functools.partial(adam_kernel, side=side, own=own), grid=(...  114 us
  transfers between devices with their start and end apart: 1, of which 0 were waited for; matrix products, arithmetic and copies ran while one was open for 0% of the time, Pallas kernels for 17%

profile of v4, /device:TPU:97, one launch (start us, length us, event | category | flops | bytes accessed | tf_op | source)
XLA Modules:
  0.0 396.9 jit_solution(14515763868715842336)
XLA Ops:
  7.2 0.1 all-gather.3.cloned.1.call-start
  7.3 268.6 %layers.1 = (bf16[12,2,2,16,32,384]{5,4,3,2,1,0:T(8,128)(2,1)}, bf16[8,2,32,384]{3,2,1,0:T(8,128)(2,1)}, f32[8,128]{1,0:T(8,128)}, f32[10,2048,256]{2,1,0:T(8,128)}, f32[10,2048,256]{2,1,0:T(8,128)}) custom-call(bf16[2048,1024]{1,0:T(8,128)(2,1)} %bitcast.4, bf16[2048,1024]{1,0:T(8,128)(2,1)} %bitcast.5, bf16[2,1024,2560]{2,1,0:T(8,128)(2,1)} %refs_0_.3, ...), custom_call_target="tpu_custom_call" | custom-call | flops 161061273600 | bytes 62914560 | tf_op jit(solution)/shard_map/layers/pallas_call | solution.py:561
  275.9 0.1 all-gather.3.cloned.1.call-update
  276.0 68.5 %adam_own.1 = (bf16[2,1024,2560]{2,1,0:T(8,128)(2,1)}, bf16[2,1024,2560]{2,1,0:T(8,128)(2,1)}, bf16[2,2560,1024]{2,1,0:T(8,128)(2,1)}, f32[2,1024,2560]{2,1,0:T(...) custom-call(f32[8,128]{1,0:T(8,128)} %get-tuple-element.21.factor_re, ...), custom_call_target="tpu_custom_call" | custom-call | flops 188743680 | bytes 207618048 | tf_op jit(solution)/shard_map/adam_own/pallas_call | solution.py:645
  344.5 0.0 all-gather.3.cloned.1.call-done
  344.5 45.5 %adam_rest.1 = (bf16[2,1024,2560]{2,1,0:T(8,128)(2,1)}, bf16[2,1024,2560]{2,1,0:T(8,128)(2,1)}, bf16[2,2560,1024]{2,1,0:T(8,128)(2,1)}, f32[2,1024,2560]{2,1,0:T...) custom-call(f32[8,128]{1,0:T(8,128)} %get-tuple-element.21.factor_re, ...), custom_call_target="tpu_custom_call", output_to_operand_aliasing={{0}: (11, {}), {1}: (12, {}), {2}: (13, {}), {3}: (14, {}),... | custom-call | flops 125829120 | bytes 138412032 | tf_op jit(solution)/shard_map/adam_rest/pallas_call | solution.py:645
Async XLA Ops:
  7.2 337.3 %all-gather.3.cloned.1.call-start = ((), (), s32[]{:S(2)}) async-start(), calls=%async_computation | async-start | bytes 12976128 | tf_op jit(solution)/shard_map/all_gather | solution.py:674
Sparse Core Ops, SparseCore 0:
  276.1 57.4 all-gather.2
